TPU v7x, 32 devices: a whole 2x2x4 slice. The times are simulated.
32 devices in a mesh: freq: 8 (over z, y), col: 4 (over x, core).
Axes of the slice: x: 2, y: 2, z: 4, core: 2. Of those that a mesh axis runs over, the one named last changes fastest.
Arguments:
- traces: bfloat16 [16, 512, 64, 512], P('col', 'freq'), may hold values from -6 to 6
- left_factors: bfloat16 [32, 16, 16, 16, 512], P('freq', None, 'col'), may hold values from -0.5 to 0.5
- right_factors: bfloat16 [32, 16, 16, 16, 512], P('freq', None, 'col'), may hold values from -0.25 to 0.25
- tile_ranks: int32 [32, 16, 16], P('freq', None, 'col'), may hold values from 1 to 16, as said below
Outputs:
- modelled: bfloat16 [16, 512, 64, 512], P('col', 'freq')
Inputs may be any that keep to these rules, and one draw needn't show every extreme that they name: `tile_ranks`: the rank of each kernel tile; factor rows at or past it are not part of the kernel. 16 is reached by some tile in every draw.
All inputs are finite; a program needn't handle non-finite values.
Results may differ from a plain program's by a relative error of at most 0.0072.
Values may be sent and summed in bfloat16 or wider, within the bound.
No kernel may reach another device: no remote copies, remote signals or barrier semaphores. Data moves between devices by JAX's collectives and lax.ppermute only.
A program may use at most 128 MiB of HBM per device.

v0:
```python
import jax
import jax.numpy as jnp
from jax import lax
from jax.sharding import PartitionSpec as P


def hartley_table(time_count, freq_count):
    times = jnp.arange(time_count, dtype=jnp.int32)
    freqs = jnp.arange(freq_count, dtype=jnp.int32)
    phase = times[:, None] * freqs[None, :] % time_count
    angle = 2.0 * jnp.pi / time_count * phase.astype(jnp.float32)
    scale = jnp.sqrt(jnp.float32(time_count))
    return ((jnp.cos(angle) + jnp.sin(angle)) / scale).astype(jnp.bfloat16)


def tile_coeffs(spectrum, right_tiles, rank_tiles):
    coeffs = jnp.einsum("cws,rcks->rwck", spectrum, right_tiles, preferred_element_type=jnp.float32)
    kept_mask = (
        lax.broadcasted_iota(jnp.int32, (1, 1, 1, right_tiles.shape[2]), 3)
        < rank_tiles[:, None, :, None]
    )
    return jnp.where(kept_mask, coeffs, 0.0).astype(jnp.bfloat16)


def shards(traces, left_factors, right_factors, tile_ranks):
    freq_local = left_factors.shape[0]
    cas_table = hartley_table(traces.shape[3], freq_local * lax.axis_size("freq"))
    left_rows = lax.all_to_all(left_factors, "col", split_axis=1, concat_axis=2, tiled=True)
    spectra_local = jnp.einsum(
        "cswt,tk->kcws", traces, cas_table, preferred_element_type=jnp.float32
    ).astype(jnp.bfloat16)

    def frequency_coeffs(spectrum, right_tiles, rank_tiles):
        return tile_coeffs(spectrum, right_tiles, rank_tiles)

    spec_items = lax.all_to_all(spectra_local, "freq", split_axis=0, concat_axis=3, tiled=True)
    exchanged = jnp.stack(
        [
            frequency_coeffs(spec_items[index], right_factors[index], tile_ranks[index])
            for index in range(freq_local)
        ]
    )
    coeff_rows = lax.all_to_all(exchanged, "col", split_axis=1, concat_axis=3, tiled=True)
    synthesis = jnp.einsum(
        "frwck,frcks->frws", coeff_rows, left_rows, preferred_element_type=jnp.float32
    ).astype(jnp.bfloat16)
    return jnp.einsum(
        "krws,tk->rswt",
        lax.all_to_all(synthesis, "freq", split_axis=3, concat_axis=0, tiled=True),
        cas_table,
        preferred_element_type=jnp.float32,
    ).astype(jnp.bfloat16)


def solution(mesh):
    in_specs = (
        P("col", "freq", None, None),
        P("freq", None, "col", None, None),
        P("freq", None, "col", None, None),
        P("freq", None, "col"),
    )
    out_specs = P("col", "freq", None, None)
    return jax.shard_map(shards, mesh=mesh, in_specs=in_specs, out_specs=out_specs, check_vma=False)
```

profile of v0, /device:TPU:0, one launch (start us, length us, event | category | flops | bytes accessed | tf_op | source)
XLA Modules:
  0.0 203.0 jit_solution(1279327411745509153)
XLA Ops:
  0.0 12.0 %convert_bitcast_fusion.1 = bf16[32,4,64,64]{2,0,3,1:T(8,128)(2,1)S(1)} fusion(bf16[4,64,64,512]{3,2,1,0:T(8,128)(2,1)} %param.4), kind=kOutput, calls=%fused_computation.2 | convolution fusion | flops 537673728 | bytes 17825792 | tf_op jit(solution)/shard_map/cswt,tk->kcws/dot_general | solution.py:29
  12.0 0.0 copy-start.3
  12.0 0.8 copy.50
  12.8 2.7 %reshape.48 = bf16[8,2,32768]{2,1,0:T(2,128)(2,1)} reshape(bf16[32,4,64,64]{3,2,1,0:T(8,128)(2,1)S(1)} %bitcast.124) | data formatting | bytes 2097152
  15.5 7.3 %all-to-all-start = ((bf16[8,2,32768]{2,1,0:T(2,128)(2,1)}), bf16[8,2,32768]{2,1,0:T(2,128)(2,1)S(1)}, u32[]{:S(2)}, u32[]{:S(2)}) async-start(bf16[8,2,32768]{2,1,0:T(2,128)(2,1)} %reshape.48), calls=%async_computation | async-start | bytes 2097152 | tf_op jit(solution)/shard_map/all_to_all | solution.py:36
  22.8 0.0 copy-done.3
  22.8 0.1 iota_compare_fusion.2
  22.9 0.1 iota_compare_fusion
  23.0 4.4 %fusion.41 = (bf16[1,16,4,16,512]{4,3,2,1,0:T(8,128)(2,1)}, bf16[1,16,4,16,512]{4,3,2,1,0:T(8,128)(2,1)}, bf16[1,16,4,16,512]{4,3,2,1,0:T(8,128)(2,1)}, bf16[1,16,4,16,512]{4,3,2,1,0:T(8,128)(2,1)}) fusion(bf16[4,16,4,16,512]{4,3,2,1,0:T(8,128)(2,1)} %param.6), kind=kLoop, calls=%fused_computation.63 | loop fusion | bytes 8388608 | tf_op jit(solution)/shard_map/slice | solution.py:39
  27.4 21.1 %all-to-all-done = bf16[8,2,32768]{2,1,0:T(2,128)(2,1)S(1)} async-done(((bf16[8,2,32768]{2,1,0:T(2,128)(2,1)}), bf16[8,2,32768]{2,1,0:T(2,128)(2,1)S(1)}, u32[]{:S(2)}, u32[]{:S(2)}) %all-to-all-start) | async-done | bytes 1048608 | tf_op jit(solution)/shard_map/all_to_all | solution.py:36
  48.5 2.7 %reshape.49 = bf16[32,4,64,64]{3,2,1,0:T(8,128)(2,1)} reshape(bf16[8,2,32768]{2,1,0:T(2,128)(2,1)S(1)} %all-to-all-done) | data formatting | bytes 2097152
  51.2 3.1 %copy.18 = bf16[8,4,4,64,64]{4,0,3,2,1:T(8,128)(2,1)S(1)} copy(bf16[8,4,4,64,64]{3,4,2,1,0:T(8,128)(2,1)} %bitcast.125) | data formatting | bytes 2097152 | tf_op jit(solution)/shard_map/all_to_all | solution.py:36
  54.3 1.1 fusion.42
  55.4 0.0 copy-start.1
  55.4 2.2 %reshape.39 = bf16[4,64,512,1]{2,1,0,3:T(8,128)(2,1)} reshape(bf16[1,4,64,8,64]{4,3,2,1,0:T(8,128)(2,1)} %get-tuple-element.9) | data formatting | bytes 524288 | tf_op jit(solution)/shard_map/squeeze | solution.py:39
  57.6 2.1 %reshape.42 = bf16[4,64,512,1]{2,1,0,3:T(8,128)(2,1)} reshape(bf16[1,4,64,8,64]{4,3,2,1,0:T(8,128)(2,1)} %get-tuple-element.10) | data formatting | bytes 524288 | tf_op jit(solution)/shard_map/squeeze | solution.py:39
  59.7 0.0 copy-start
  59.7 0.3 reshape.41
  60.0 0.0 copy-start.2
  60.0 0.3 reshape.40
  60.4 1.7 fusion.8
  62.1 1.6 fusion.10
  63.8 0.0 copy-done.1
  63.8 0.0 copy-done.2
  63.8 0.4 fusion.11
  64.2 0.0 copy-done
  64.2 0.4 fusion.9
  64.6 0.3 copy_bitcast_fusion.9
  64.9 1.6 reshape.50
  66.5 3.5 %all-to-all-start.1 = ((bf16[4,2,32768]{2,1,0:T(2,128)(2,1)}), bf16[4,2,32768]{2,1,0:T(2,128)(2,1)S(1)}, u32[]{:S(2)}, u32[]{:S(2)}) async-start(bf16[4,2,32768]{2,1,0:T(2,128)(2,1)} %reshape.50), calls=%async_computation.1 | async-start | bytes 1048576 | tf_op jit(solution)/shard_map/all_to_all | solution.py:43
  70.0 5.0 %copy.25 = bf16[4,16,4,16,512]{4,3,2,0,1:T(8,128)(2,1)} copy(bf16[4,16,4,16,512]{4,3,2,1,0:T(8,128)(2,1)} %param.5) | data formatting | bytes 8388608 | tf_op args[1]
  75.0 3.8 %all-to-all-done.1 = bf16[4,2,32768]{2,1,0:T(2,128)(2,1)S(1)} async-done(((bf16[4,2,32768]{2,1,0:T(2,128)(2,1)}), bf16[4,2,32768]{2,1,0:T(2,128)(2,1)S(1)}, u32[]{:S(2)}, u32[]{:S(2)}) %all-to-all-start.1) | async-done | bytes 524320 | tf_op jit(solution)/shard_map/all_to_all | solution.py:43
  78.8 4.9 %all-to-all-start.2 = ((bf16[4,16,4,16,512]{4,3,2,0,1:T(8,128)(2,1)}), bf16[4,16,4,16,512]{4,3,2,0,1:T(8,128)(2,1)}, u32[]{:S(2)}, u32[]{:S(2)}) async-start(bf16[4,16,4,16,512]{4,3,2,0,1:T(8,128)(2,1)} %copy.25), calls=%async_computation.2 | async-start | bytes 8388608 | tf_op jit(solution)/shard_map/all_to_all | solution.py:28
  83.6 0.7 reshape.51
  84.4 0.2 copy.24
  84.6 47.2 %all-to-all-done.2 = bf16[4,16,4,16,512]{4,3,2,0,1:T(8,128)(2,1)} async-done(((bf16[4,16,4,16,512]{4,3,2,0,1:T(8,128)(2,1)}), bf16[4,16,4,16,512]{4,3,2,0,1:T(8,128)(2,1)}, u32[]{:S(2)}, u32[]{:S(2)}) %all-to-all-start.2) | async-done | bytes 4194336 | tf_op jit(solution)/shard_map/all_to_all | solution.py:28
  131.8 2.7 %copy.26 = bf16[4,4,4,4,16,512]{5,4,3,1,2,0:T(8,128)(2,1)S(1)} copy(bf16[4,4,4,4,16,512]{5,4,3,0,2,1:T(8,128)(2,1)} %bitcast.29) | data formatting | bytes 8388608 | tf_op jit(solution)/shard_map/all_to_all | solution.py:28
  134.5 0.9 bitcast_convert_fusion
  135.4 1.9 copy.27
  137.3 1.7 reshape.52
  139.0 28.9 %all_to_all.69 = bf16[8,2,32768]{2,1,0:T(2,128)(2,1)S(1)} all-to-all(bf16[8,2,32768]{2,1,0:T(2,128)(2,1)S(1)} %reshape.52), channel_id=1, replica_groups=mesh['freq'=8,'col'=4] {'freq'}, dimensions={0} | all-to-all | bytes 2097152 | tf_op jit(solution)/shard_map/all_to_all | solution.py:49
  167.9 2.7 %reshape.53 = bf16[512,4,4,64]{3,2,1,0:T(4,128)(2,1)} reshape(bf16[8,2,32768]{2,1,0:T(2,128)(2,1)S(1)} %all_to_all.69) | data formatting | bytes 2097152
  170.6 5.6 %copy.28 = bf16[4,4,64,8,64]{4,0,3,2,1:T(4,128)(2,1)S(1)} copy(bf16[4,4,64,8,64]{2,1,0,4,3:T(4,128)(2,1)} %bitcast.126) | data formatting | bytes 2097152 | tf_op jit(solution)/shard_map/all_to_all | solution.py:49
  176.1 8.4 %convert_bitcast_fusion = bf16[4,64,64,512]{3,1,2,0:T(8,128)(2,1)} fusion(bf16[32,4,64,64]{3,0,2,1:T(8,128)(2,1)S(1)} %bitcast.121), kind=kOutput, calls=%fused_computation | convolution fusion | flops 545538048 | bytes 17825792 | tf_op jit(solution)/shard_map/krws,tk->rswt/dot_general | solution.py:47
  184.5 18.5 %copy.29 = bf16[4,64,64,512]{3,2,1,0:T(8,128)(2,1)} copy(bf16[4,64,64,512]{3,1,2,0:T(8,128)(2,1)} %convert_bitcast_fusion) | data formatting | bytes 33554432 | tf_op jit(solution)/shard_map/convert_element_type | solution.py:52
  (1 shorter events, 0.0 us)
Async XLA Ops:
  12.0 10.8 %copy-start.3 = (s32[4,16,4]{1,2,0:T(4,128)S(1)}, s32[4,16,4]{1,2,0:T(4,128)}, u32[]{:S(2)}) copy-start(s32[4,16,4]{1,2,0:T(4,128)} %param.7) | copy-start | bytes 3076
  15.5 33.1 %all-to-all-start = ((bf16[8,2,32768]{2,1,0:T(2,128)(2,1)}), bf16[8,2,32768]{2,1,0:T(2,128)(2,1)S(1)}, u32[]{:S(2)}, u32[]{:S(2)}) async-start(bf16[8,2,32768]{2,1,0:T(2,128)(2,1)} %reshape.48), calls=%async_computation | async-start | bytes 2097152 | tf_op jit(solution)/shard_map/all_to_all | solution.py:36
  55.4 8.3 %copy-start.1 = (bf16[1,16,4,16,512]{4,3,2,1,0:T(8,128)(2,1)S(1)}, bf16[1,16,4,16,512]{4,3,2,1,0:T(8,128)(2,1)}, u32[]{:S(2)}) copy-start(bf16[1,16,4,16,512]{4,3,2,1,0:T(8,128)(2,1)} %get-tuple-element.5) | copy-start | bytes 3145732
  59.7 4.5 %copy-start = (bf16[1,16,4,16,512]{4,3,2,1,0:T(8,128)(2,1)S(1)}, bf16[1,16,4,16,512]{4,3,2,1,0:T(8,128)(2,1)}, u32[]{:S(2)}) copy-start(bf16[1,16,4,16,512]{4,3,2,1,0:T(8,128)(2,1)} %get-tuple-element.6) | copy-start | bytes 3145732
  60.0 3.7 %copy-start.2 = (bf16[4,64,512,1]{2,1,0,3:T(8,128)(2,1)S(1)}, bf16[4,64,512,1]{2,1,0,3:T(8,128)(2,1)}, u32[]{:S(2)}) copy-start(bf16[4,64,512,1]{2,1,0,3:T(8,128)(2,1)} %reshape.39) | copy-start | bytes 786436
  66.5 12.3 %all-to-all-start.1 = ((bf16[4,2,32768]{2,1,0:T(2,128)(2,1)}), bf16[4,2,32768]{2,1,0:T(2,128)(2,1)S(1)}, u32[]{:S(2)}, u32[]{:S(2)}) async-start(bf16[4,2,32768]{2,1,0:T(2,128)(2,1)} %reshape.50), calls=%async_computation.1 | async-start | bytes 1048576 | tf_op jit(solution)/shard_map/all_to_all | solution.py:43
  78.8 53.1 %all-to-all-start.2 = ((bf16[4,16,4,16,512]{4,3,2,0,1:T(8,128)(2,1)}), bf16[4,16,4,16,512]{4,3,2,0,1:T(8,128)(2,1)}, u32[]{:S(2)}, u32[]{:S(2)}) async-start(bf16[4,16,4,16,512]{4,3,2,0,1:T(8,128)(2,1)} %copy.25), calls=%async_computation.2 | async-start | bytes 8388608 | tf_op jit(solution)/shard_map/all_to_all | solution.py:28
where the time goes:
time: 204 us; the launch traced here: 203 us
  waiting for transfers between devices  72.1 us (35%)
  local copies, waits for them, and re-layouts  60.3 us (30%)
  blocking collectives  28.9 us (14%)
  matrix products  25.4 us (12%)
  starting transfers between devices  15.6 us (8%)
    all_to_all x1, waiting for transfers between devices, shards(): lax.all_to_all(left_factors, 'col', split_axis=1, concat_axis=2, tiled=True)  47.2 us
    all_to_all x1, blocking collectives, shards(): lax.all_to_all(synthesis, 'freq', split_axis=3, concat_axis=0, tiled=True)  28.9 us
    all_to_all x1, waiting for transfers between devices, shards(): lax.all_to_all(spectra_local, 'freq', split_axis=0, concat_axis=3, tiled=...  21.1 us
    convert_element_type x1, local copies, waits for them, and re-layouts, shards(): return jnp.einsum('krws,tk->rswt', lax.all_to_all(synthesis, 'freq', spli...  18.5 us
    unnamed x15, local copies, waits for them, and re-layouts  17 us
    dot_general x1, matrix products, shards(): jnp.einsum('cswt,tk->kcws', traces, cas_table, preferred_element_type=jnp...  12 us
    dot_general x1, matrix products, shards(): jnp.einsum('krws,tk->rswt', lax.all_to_all(synthesis, 'freq', split_axis=...  8.42 us
    all_to_all x1, starting transfers between devices, shards(): lax.all_to_all(spectra_local, 'freq', split_axis=0, concat_axis=3, tiled=...  7.31 us
  transfers between devices with their start and end apart: 3, of which 3 were waited for; matrix products, arithmetic and copies ran while one was open for 5% of the time, Pallas kernels for 0%

commit v1 on v0

v1 whole, which is shorter than its diff:
```python
import functools

import jax
import jax.numpy as jnp
import numpy as np
from jax import lax
from jax.experimental import pallas as pl
from jax.experimental.pallas import tpu as pltpu
from jax.sharding import PartitionSpec as P

LANES = 128
WIDE = 58 << 20
ROWS = 16


def hartley_table(time_count, freq_count):
    phase = np.arange(time_count)[:, None] * np.arange(freq_count)[None, :] % time_count
    angle = np.float32(2.0 * np.pi / time_count) * phase.astype(np.float32)
    table = (np.cos(angle) + np.sin(angle)) / np.sqrt(np.float32(time_count))
    return table.astype(np.float32).astype(jnp.bfloat16)


def forward_kernel(x_ref, cas_ref, *refs, shares, depth, group):
    spectra, (buffer, held, arrived) = refs[:shares], refs[shares:]
    steps, pack, count, _, _ = buffer.shape
    all_freqs = cas_ref.shape[0]
    freqs = all_freqs // shares
    across = x_ref.shape[1] // count
    place = lax.axis_index("freq")

    def copies(step):
        first = pl.multiple_of(step % across * count, count)
        return [
            pltpu.make_async_copy(
                x_ref.at[step // across * pack + c, pl.ds(first, count)], buffer.at[step, c], arrived.at[step, c]
            )
            for c in range(pack)
        ]

    for step in range(min(depth, steps)):
        for copy in copies(step):
            copy.start()

    def body(step, carry):
        for copy in copies(step):
            copy.wait()

        @pl.when(step + depth < steps)
        def _():
            for copy in copies(step + depth):
                copy.start()

        for s in range(0, count, group):
            rows = jnp.concatenate([buffer[step, c, s + i] for i in range(group) for c in range(pack)], axis=0)
            product = lax.dot_general(
                cas_ref[...], rows, (((1,), (1,)), ((), ())), preferred_element_type=jnp.float32
            )
            for i in range(group):
                held[(s + i) * all_freqs : (s + i + 1) * all_freqs, :] = product[:, i * LANES : (i + 1) * LANES]
        first = pl.multiple_of(step % across * count, count)
        for shift in range(shares):
            low = lax.rem(place + shift, shares) * freqs
            for k in range(freqs):
                spectra[shift][k, step // across, pl.ds(first, count), :] = held[
                    pl.ds(low + k, count, stride=all_freqs), :
                ].astype(jnp.bfloat16)
        return carry

    lax.fori_loop(0, steps, body, 0)


def forward(traces, cas, shares):
    tiles, sources, waves, times = traces.shape
    all_freqs = cas.shape[0]
    freqs = all_freqs // shares
    pack = LANES // waves
    count = min(ROWS, sources)
    steps = tiles // pack * (sources // count)
    vmem = pl.BlockSpec(memory_space=pltpu.VMEM)
    return pl.pallas_call(
        functools.partial(forward_kernel, shares=shares, depth=4, group=4),
        out_shape=[jax.ShapeDtypeStruct((freqs, tiles // pack, sources, LANES), jnp.bfloat16)] * shares,
        in_specs=[pl.BlockSpec(memory_space=pltpu.HBM), vmem],
        out_specs=[vmem] * shares,
        scratch_shapes=[
            pltpu.VMEM((steps, pack, count, waves, times), jnp.bfloat16),
            pltpu.VMEM((count * all_freqs, LANES), jnp.float32),
            pltpu.SemaphoreType.DMA((steps, pack)),
        ],
        cost_estimate=pl.CostEstimate(
            flops=2 * traces.size * all_freqs, bytes_accessed=2 * traces.size, transcendentals=0
        ),
        name="forward",
    )(traces, cas)


def stage_kernel(*refs, count, pieces):
    operands, outputs, arrived = refs[:count], refs[count:-1], refs[-1]
    me = lax.axis_index("col")
    copies = [
        pltpu.make_async_copy(
            operands[operand] if take is None else operands[operand].at[:, pl.ds(take(me), wide)],
            outputs[output] if put is None else outputs[output].at[:, put],
            arrived.at[i],
        )
        for i, (operand, output, take, wide, put) in enumerate(pieces)
    ]
    for copy in copies:
        copy.start()
    for copy in copies:
        copy.wait()


def stage(operands, shapes, pieces, grant):
    return pl.pallas_call(
        functools.partial(stage_kernel, count=len(operands), pieces=pieces),
        out_shape=[jax.ShapeDtypeStruct(shape, jnp.bfloat16) for shape in shapes],
        in_specs=[pl.BlockSpec(memory_space=pltpu.HBM)] * len(operands),
        out_specs=[pl.BlockSpec(memory_space=pltpu.VMEM)] * len(shapes),
        scratch_shapes=[pltpu.SemaphoreType.DMA((len(pieces),))],
        cost_estimate=pl.CostEstimate(flops=1 << 28, bytes_accessed=1 << 22, transcendentals=0),
        compiler_params=pltpu.CompilerParams(vmem_limit_bytes=grant),
        name="stage",
    )(*operands)


def coeff_kernel(ranks_ref, right_ref, *refs, shares, owners, inner):
    spectra, direct = refs[:shares], refs[shares : shares + owners]
    paired, (spec_ref, rows_ref, right_held, own_held, arrived) = refs[shares + owners : -5], refs[-5:]
    freqs, receivers, tiles, ranks, sources = right_ref.shape
    own = pltpu.make_async_copy(spectra[0], own_held, arrived.at[freqs])
    own.start()
    for k in range(freqs):
        pltpu.make_async_copy(right_ref.at[k], right_held.at[k], arrived.at[k]).start()
    spectra = [own_held] + list(spectra[1:])
    pairs, each = spectra[0].shape[1:3]
    pack = tiles // pairs
    waves = LANES // pack
    me, place = lax.axis_index("col"), lax.axis_index("freq")
    lane_tile = lax.broadcasted_iota(jnp.int32, (ranks, LANES), 1) // waves
    rank_row = lax.broadcasted_iota(jnp.int32, (ranks, LANES), 0)
    per_owner = receivers // owners

    own.wait()

    def body(k, carry):
        pltpu.make_async_copy(right_ref.at[k], right_held.at[k], arrived.at[k]).wait()
        for pair in range(pairs):
            for shift in range(shares):
                first = pl.multiple_of(lax.rem(place + shares - shift, shares) * each, each)
                spec_ref[pair, pl.ds(first, each), :] = spectra[shift][k, pair]
        for pair in range(pairs):
            product = [
                jnp.dot(
                    right_held[k, :, pair * pack + h].reshape(receivers * ranks, sources),
                    spec_ref[pair],
                    preferred_element_type=jnp.float32,
                )
                for h in range(pack)
            ]
            for r in range(receivers):
                entry = (k * receivers + r) * tiles + pair * pack
                kept = product[0][r * ranks : (r + 1) * ranks]
                limit = jnp.full((ranks, LANES), ranks_ref[entry], jnp.int32)
                for h in range(1, pack):
                    here = lane_tile == h
                    kept = jnp.where(here, product[h][r * ranks : (r + 1) * ranks], kept)
                    limit = jnp.where(here, ranks_ref[entry + h], limit)
                kept = jnp.where(rank_row < limit, kept, 0.0)
                rows_ref[pair, r] = kept.astype(jnp.bfloat16)
            for shift in range(owners):
                first = lax.rem(me + shift, owners) * per_owner
                for i in range(pack):
                    direct[shift][k, pair, i * ranks : (i + 1) * ranks, :] = rows_ref[pair, first + i]
            for side in range(inner):
                core = lax.rem(me + side, inner)
                for outer in range(owners // inner):
                    first = (outer * inner + core) * per_owner + pack
                    for i in range(pack):
                        paired[side][k, outer, pair, i * ranks : (i + 1) * ranks, :] = rows_ref[pair, first + i]
        return carry

    lax.fori_loop(0, freqs, body, 0)


def coefficients(ranks, spectra, right, owners, inner):
    freqs, receivers, tiles, rank_count, sources = right.shape
    shares = len(spectra)
    pairs = spectra[0].shape[1]
    rows = tiles // pairs * rank_count
    outer = owners // inner
    vmem, smem = pl.BlockSpec(memory_space=pltpu.VMEM), pl.BlockSpec(memory_space=pltpu.SMEM)
    anywhere = pl.BlockSpec(memory_space=pl.ANY)
    return pl.pallas_call(
        functools.partial(coeff_kernel, shares=shares, owners=owners, inner=inner),
        out_shape=[jax.ShapeDtypeStruct((freqs, pairs, rows, LANES), jnp.bfloat16)] * owners
        + [jax.ShapeDtypeStruct((freqs, outer, pairs, rows, LANES), jnp.bfloat16)] * inner,
        in_specs=[smem, anywhere, anywhere] + [vmem] * (shares - 1),
        out_specs=[vmem] * (owners + inner),
        scratch_shapes=[
            pltpu.VMEM((pairs, sources, LANES), jnp.bfloat16),
            pltpu.VMEM((pairs, receivers, rank_count, LANES), jnp.bfloat16),
            pltpu.VMEM(right.shape, jnp.bfloat16),
            pltpu.VMEM(spectra[0].shape, jnp.bfloat16),
            pltpu.SemaphoreType.DMA((freqs + 1,)),
        ],
        cost_estimate=pl.CostEstimate(
            flops=2 * right.size * LANES, bytes_accessed=2 * right.size, transcendentals=0
        ),
        compiler_params=pltpu.CompilerParams(vmem_limit_bytes=WIDE),
        name="coefficients",
    )(ranks.reshape(-1), right, *spectra)


def synthesis_kernel(*refs, count, chip, added):
    coeff_refs, left_refs = refs[:count], refs[count : 2 * count]
    freqs = left_refs[0].shape[0]
    pack, tiles, ranks, sources = left_refs[0].shape[-4:]
    waves = LANES // pack
    place = lax.axis_index("freq")
    here = None if chip is None else chip(lax.axis_index("col"))
    outputs = refs[2 * count + added :]
    turned = len(outputs) > 1
    if turned:
        outputs, turned_ref = outputs[:-1], outputs[-1]
        shares = len(outputs)
        each = sources // shares

    def pick(ref, k, rank):
        if len(ref.shape) == rank + 1:
            return ref.at[k]
        return ref.at[k, ref.shape[1] - 1 if here is None else here]

    for k in range(freqs):
        parts = []
        for r in range(pack):
            weights = jnp.concatenate(
                [
                    pick(ref, k, 3)[
                        c // pack, r * ranks : (r + 1) * ranks, c % pack * waves : (c % pack + 1) * waves
                    ]
                    for ref in coeff_refs
                    for c in range(tiles)
                ],
                axis=0,
            )
            left = jnp.concatenate([pick(ref, k, 4)[r].reshape(tiles * ranks, sources) for ref in left_refs], axis=0)
            part = lax.dot_general(weights, left, (((0,), (0,)), ((), ())), preferred_element_type=jnp.float32)
            if added:
                part = part + refs[2 * count][k, r].astype(jnp.float32)
            parts.append(part.astype(jnp.bfloat16))
        if turned:
            turned_ref[k] = jnp.concatenate(parts, axis=0).T
            for shift in range(shares):
                first = pl.multiple_of(lax.rem(place + shift, shares) * each, each)
                outputs[shift][k] = turned_ref[k, pl.ds(first, each), :]
        else:
            for r in range(pack):
                outputs[0][k, r] = parts[r]


def synthesis(coeffs, lefts, added, shares, waves, chip):
    pack = LANES // waves
    freqs = coeffs[0].shape[0]
    tiles, rank_count, sources = lefts[0].shape[-3:]
    vmem = pl.BlockSpec(memory_space=pltpu.VMEM)
    if shares:
        out_shape = [jax.ShapeDtypeStruct((freqs, sources // shares, LANES), jnp.bfloat16)] * shares
        scratch = [pltpu.VMEM((freqs, sources, LANES), jnp.bfloat16)]
    else:
        out_shape = [jax.ShapeDtypeStruct((freqs, pack, waves, sources), jnp.bfloat16)]
        scratch = []
    extra = [] if added is None else [added]
    flops = 2 * freqs * pack * waves * sources * tiles * rank_count * len(coeffs)
    return pl.pallas_call(
        functools.partial(synthesis_kernel, count=len(coeffs), chip=chip, added=len(extra)),
        out_shape=out_shape,
        in_specs=[vmem] * (2 * len(coeffs) + len(extra)),
        out_specs=[vmem] * len(out_shape),
        scratch_shapes=scratch,
        cost_estimate=pl.CostEstimate(flops=flops, bytes_accessed=flops // waves, transcendentals=0),
        compiler_params=pltpu.CompilerParams(vmem_limit_bytes=8 << 20),
        name="synthesis",
    )(*coeffs, *lefts, *extra)


def inverse_kernel(cas_ref, *refs, shares, group):
    syn_refs = refs[:shares]
    out_ref, buffer, held, left = refs[-4:]
    steps, pack, count, waves, _ = buffer.shape
    freqs = cas_ref.shape[0]
    rows = freqs // shares * count
    place = lax.axis_index("freq")

    def copies(step):
        first = pl.multiple_of(step * count, count)
        return [
            pltpu.make_async_copy(
                buffer.at[step, r], out_ref.at[group * pack + r, pl.ds(first, count)], left.at[step, r]
            )
            for r in range(pack)
        ]

    def body(step, carry):
        first = pl.multiple_of(step * count, count)
        for shift in range(shares):
            low = pl.multiple_of(lax.rem(place + shares - shift, shares) * rows, rows)
            held[pl.ds(low, rows), :] = (
                syn_refs[shift][:, pl.ds(first, count), :].astype(jnp.float32).reshape(rows, LANES)
            )
        for s in range(count):
            weights = held[pl.ds(s, freqs, stride=count), :].astype(jnp.bfloat16)
            block = lax.dot_general(
                weights, cas_ref[...], (((0,), (0,)), ((), ())), preferred_element_type=jnp.float32
            ).astype(jnp.bfloat16)
            for r in range(pack):
                buffer[step, r, s] = block[r * waves : (r + 1) * waves]
        for copy in copies(step):
            copy.start()
        return carry

    lax.fori_loop(0, steps, body, 0)
    for step in range(steps):
        for copy in copies(step):
            copy.wait()


def inverse(synthesised, cas, waves, group, groups, partial):
    shares = len(synthesised)
    _, sources, _ = synthesised[0].shape
    freqs, times = cas.shape
    pack = LANES // waves
    count = min(ROWS, sources)
    steps = sources // count
    vmem = pl.BlockSpec(memory_space=pltpu.VMEM)
    extra = [] if partial is None else [partial]
    return pl.pallas_call(
        functools.partial(inverse_kernel, shares=shares, group=group),
        out_shape=jax.ShapeDtypeStruct((groups * pack, sources, waves, times), jnp.bfloat16),
        in_specs=[vmem] + [vmem] * shares + [pl.BlockSpec(memory_space=pltpu.HBM)] * len(extra),
        out_specs=pl.BlockSpec(memory_space=pltpu.HBM),
        scratch_shapes=[
            pltpu.VMEM((steps, pack, count, waves, times), jnp.bfloat16),
            pltpu.VMEM((freqs * count, LANES), jnp.float32),
            pltpu.SemaphoreType.DMA((steps, pack)),
        ],
        input_output_aliases={1 + shares: 0} if extra else {},
        cost_estimate=pl.CostEstimate(
            flops=2 * sources * LANES * times * freqs,
            bytes_accessed=2 * sources * LANES * times,
            transcendentals=0,
        ),
        compiler_params=pltpu.CompilerParams(vmem_limit_bytes=14 << 20),
        name="inverse",
    )(cas, *synthesised, *extra)


def shards(traces, left_factors, right_factors, tile_ranks):
    shares, owners = lax.axis_size("freq"), lax.axis_size("col")
    inner = 2
    outer = owners // inner
    freq_local, receivers = left_factors.shape[:2]
    tile = left_factors.shape[2:]
    waves = traces.shape[2]
    pack = LANES // waves
    per_owner = receivers // owners
    groups = per_owner // pack
    cas = jnp.asarray(hartley_table(traces.shape[3], freq_local * shares).T)

    def shifted(block, shift, axis, size):
        return lax.ppermute(block, axis, [(i, (i + shift) % size) for i in range(size)])

    def exchanged(blocks, axis):
        size = len(blocks)
        arrived = [blocks[0]] + [None] * (size - 1)
        for shift in start_order(size):
            arrived[shift] = shifted(blocks[shift], shift, axis, size)
        return arrived

    def swapped(block, bit):
        return lax.ppermute(block, "col", [(i, i ^ bit) for i in range(owners)])

    made = list(forward(traces, cas, shares))

    def direct_first(shift):
        return lambda me: lax.rem(me + shift, owners) * per_owner

    def paired_first(side, chip):
        return lambda me: (chip * inner + lax.rem(me + side, inner)) * per_owner + pack

    direct_shape = (freq_local, pack) + tile
    paired_shape = (freq_local, outer, pack) + tile
    left_direct = stage(
        [left_factors],
        [direct_shape] * (owners - 1),
        [(0, shift - 1, direct_first(shift), pack, None) for shift in range(1, owners)],
        WIDE,
    )
    left_own, left_other = stage(
        [left_factors],
        [(freq_local, outer + 1, pack) + tile, paired_shape],
        [(0, side, paired_first(side, chip), pack, chip) for side in (1, 0) for chip in range(outer)]
        + [(0, 0, direct_first(0), pack, outer)],
        12 << 20,
    )
    spectra = exchanged(made, "freq")
    left_direct = exchanged([left_own] + list(left_direct), "col")
    left_paired = [left_own, swapped(left_other, 1)]

    made = list(coefficients(tile_ranks, spectra, right_factors, owners, inner))
    paired = [made[-2], swapped(made[-1], 1)]
    direct = exchanged(made[:owners], "col")
    (sent,) = synthesis(paired, left_paired, None, 0, waves, lambda me: (me ^ inner) // inner)
    added = swapped(sent, inner)
    first = list(synthesis(direct, left_direct, None, shares, waves, None))
    first = exchanged(first, "freq")
    second = list(synthesis(paired, left_paired, added, shares, waves, lambda me: me // inner))
    second = exchanged(second, "freq")
    modelled = inverse(first, cas, waves, 0, groups, None)
    return inverse(second, cas, waves, 1, groups, modelled)


def start_order(size):
    return sorted(range(1, size), key=lambda shift: (abs(2 * shift - size), shift))


def solution(mesh):
    in_specs = (
        P("col", "freq", None, None),
        P("freq", None, "col", None, None),
        P("freq", None, "col", None, None),
        P("freq", None, "col"),
    )
    out_specs = P("col", "freq", None, None)
    return jax.shard_map(shards, mesh=mesh, in_specs=in_specs, out_specs=out_specs, check_vma=False)
```

time: 204 us -> 133 us (0.65)
  local copies, waits for them, and re-layouts: 60.3 us -> 4.75 us
  Pallas kernels: 0 us -> 30.1 us
  starting transfers between devices: 15.6 us -> 44.9 us
  blocking collectives: 28.9 us -> 0 us
  matrix products: 25.4 us -> 0 us
  waiting for transfers between devices: 72.1 us -> 52.7 us
    all_to_all x3 -> x0, waiting for transfers between devices: 72.1 us -> none  [the longest x1 47.2 us: shards(): lax.all_to_all(left_factors, 'col', split_axis=1, concat_axis=2, tiled=True)]
    ppermute x0 -> x30, waiting for transfers between devices: none -> 52.7 us  [the longest x27 52.7 us: shifted(): lax.ppermute(block, axis, [(i, (i + shift) % size) for i in range(size)])]
    ppermute x0 -> x30, starting transfers between devices: none -> 44.9 us  [the longest x27 43.7 us: shifted(): lax.ppermute(block, axis, [(i, (i + shift) % size) for i in range(size)])]
    pallas_call x0 -> x9, Pallas kernels: none -> 30.1 us  [the longest x1 10.4 us: forward(): pl.pallas_call(functools.partial(forward_kernel, shares=shares, depth=4,...]
    all_to_all x1 -> x0, blocking collectives: 28.9 us -> none  [shards(): lax.all_to_all(synthesis, 'freq', split_axis=3, concat_axis=0, tiled=True)]
    dot_general x7 -> x0, matrix products: 25.4 us -> none  [the longest x1 12 us: shards(): jnp.einsum('cswt,tk->kcws', traces, cas_table, preferred_element_type=jnp...]
    convert_element_type x3 -> x0, local copies, waits for them, and re-layouts: 21.2 us -> none  [the longest x1 18.5 us: shards(): return jnp.einsum('krws,tk->rswt', lax.all_to_all(synthesis, 'freq', spli...]
    all_to_all x3 -> x0, starting transfers between devices: 15.6 us -> none  [the longest x1 7.31 us: shards(): lax.all_to_all(spectra_local, 'freq', split_axis=0, concat_axis=3, tiled=...]
  transfers between devices with their start and end apart: 3 -> 30, of which waited for: 3 -> 9; matrix products, arithmetic and copies ran while one was open for 5% -> 1% of each run, Pallas kernels for 0% -> 18%
where the time goes in v1:
time: 133 us
  waiting for transfers between devices  52.7 us (40%)
  starting transfers between devices  44.9 us (34%)
  Pallas kernels  30.1 us (23%)
  local copies, waits for them, and re-layouts  4.75 us (4%)
    ppermute x27, waiting for transfers between devices, shifted(): lax.ppermute(block, axis, [(i, (i + shift) % size) for i in range(size)])  52.7 us
    ppermute x27, starting transfers between devices, shifted(): lax.ppermute(block, axis, [(i, (i + shift) % size) for i in range(size)])  43.7 us
    pallas_call x1, Pallas kernels, forward(): pl.pallas_call(functools.partial(forward_kernel, shares=shares, depth=4,...  10.4 us
    pallas_call x2, Pallas kernels, inverse(): pl.pallas_call(functools.partial(inverse_kernel, shares=shares, group=gro...  8.86 us
    pallas_call x1, Pallas kernels, coefficients(): pl.pallas_call(functools.partial(coeff_kernel, shares=shares, owners=owne...  5.29 us
    unnamed x23, local copies, waits for them, and re-layouts  4.06 us
    pallas_call x2, Pallas kernels, stage(): pl.pallas_call(functools.partial(stage_kernel, count=len(operands), piece...  3.76 us
  transfers between devices with their start and end apart: 30, of which 9 were waited for; matrix products, arithmetic and copies ran while one was open for 1% of the time, Pallas kernels for 18%

profile of v1, /device:TPU:0, one launch (start us, length us, event | category | flops | bytes accessed | tf_op | source)
XLA Modules:
  0.0 132.7 jit_solution(10148181343580029278)
XLA Ops:
  0.0 2.2 %copy-done = bf16[4,16,4,16,512]{4,3,2,1,0:T(8,128)(2,1)S(1)} copy-done((bf16[4,16,4,16,512]{4,3,2,1,0:T(8,128)(2,1)S(1)}, bf16[4,16,4,16,512]{4,3,2,1,0:T(8,128)(2,1)}, u32[]{:S(2)}) %copy-start) | copy-done | bytes 4194328
  2.2 1.2 stage.2
  3.4 0.6 collective-permute-start.8
  4.0 10.4 %forward.1 = (bf16[4,2,64,128]{3,2,1,0:T(8,128)(2,1)}, bf16[4,2,64,128]{3,2,1,0:T(8,128)(2,1)}, bf16[4,2,64,128]{3,2,1,0:T(8,128)(2,1)}, bf16[4,2,64,128]{3,2,1,...) custom-call(bf16[4,64,64,512]{3,2,1,0:T(8,128)(2,1)} %x_ref.1, ...), custom_call_target="tpu_custom_call" | custom-call | flops 536870912 | bytes 16777216 | tf_op jit(solution)/shard_map/forward/pallas_call | solution.py:80
  14.4 2.6 %collective-permute-start = (bf16[4,2,64,128]{3,2,1,0:T(8,128)(2,1)}, bf16[4,2,64,128]{3,2,1,0:T(8,128)(2,1)S(1)}, u32[]{:S(2)}, u32[]{:S(2)}) collective-permute-start(bf16[4,2,64,128]{3,2,1,0:T(8,128)(2,1)} %get-tuple-element.41), channel_id=1, source_target_pairs={{0,4},{4,8},{8,12},{12,16},{16,20},{20,24},{24,28},{28,0},{1,5},{5... | collective-permute-start | bytes 393224 | tf_op jit(solution)/shard_map/ppermute | solution.py:371
  17.0 1.6 %collective-permute-start.1 = (bf16[4,2,64,128]{3,2,1,0:T(8,128)(2,1)}, bf16[4,2,64,128]{3,2,1,0:T(8,128)(2,1)S(1)}, u32[]{:S(2)}, u32[]{:S(2)}) collective-permute-start(bf16[4,2,64,128]{3,2,1,0:T(8,128)(2,1)} %get-tuple-element.42), channel_id=1, source_target_pairs={{0,8},{4,12},{8,16},{12,20},{16,24},{20,28},{24,0},{28,4},{1,9},{5... | collective-permute-start | bytes 393224 | tf_op jit(solution)/shard_map/ppermute | solution.py:371
  18.6 2.5 %collective-permute-start.2 = (bf16[4,2,64,128]{3,2,1,0:T(8,128)(2,1)}, bf16[4,2,64,128]{3,2,1,0:T(8,128)(2,1)S(1)}, u32[]{:S(2)}, u32[]{:S(2)}) collective-permute-start(bf16[4,2,64,128]{3,2,1,0:T(8,128)(2,1)} %get-tuple-element.43), channel_id=1, source_target_pairs={{0,12},{4,16},{8,20},{12,24},{16,28},{20,0},{24,4},{28,8},{1,13},{... | collective-permute-start | bytes 393224 | tf_op jit(solution)/shard_map/ppermute | solution.py:371
  21.1 1.2 collective-permute-start.3
  22.3 2.4 %collective-permute-done.refs_1_ = bf16[4,2,64,128]{3,2,1,0:T(8,128)(2,1)S(1)} collective-permute-done((bf16[4,2,64,128]{3,2,1,0:T(8,128)(2,1)}, bf16[4,2,64,128]{3,2,1,0:T(8,128)(2,1)S(1)}, u32[]{:S(2)}, u32[]{:S(2)}) %collective-permute-start) | collective-permute-done | bytes 131104 | tf_op jit(solution)/shard_map/ppermute | solution.py:371
  24.7 0.4 collective-permute-start.4
  25.1 0.3 collective-permute-done.1.refs_2_
  25.4 1.8 %collective-permute-start.5 = (bf16[4,2,64,128]{3,2,1,0:T(8,128)(2,1)}, bf16[4,2,64,128]{3,2,1,0:T(8,128)(2,1)S(1)}, u32[]{:S(2)}, u32[]{:S(2)}) collective-permute-start(bf16[4,2,64,128]{3,2,1,0:T(8,128)(2,1)} %get-tuple-element.46), channel_id=1, source_target_pairs={{0,24},{4,28},{8,0},{12,4},{16,8},{20,12},{24,16},{28,20},{1,25},{... | collective-permute-start | bytes 393224 | tf_op jit(solution)/shard_map/ppermute | solution.py:371
  27.2 8.5 %collective-permute-done.2.refs_3_ = bf16[4,2,64,128]{3,2,1,0:T(8,128)(2,1)S(1)} collective-permute-done((bf16[4,2,64,128]{3,2,1,0:T(8,128)(2,1)}, bf16[4,2,64,128]{3,2,1,0:T(8,128)(2,1)S(1)}, u32[]{:S(2)}, u32[]{:S(2)}) %collective-permute-start.2) | collective-permute-done | bytes 131104 | tf_op jit(solution)/shard_map/ppermute | solution.py:371
  35.7 5.3 %collective-permute-start.6 = (bf16[4,2,64,128]{3,2,1,0:T(8,128)(2,1)}, bf16[4,2,64,128]{3,2,1,0:T(8,128)(2,1)}, u32[]{:S(2)}, u32[]{:S(2)}) collective-permute-start(bf16[4,2,64,128]{3,2,1,0:T(8,128)(2,1)} %get-tuple-element.47), channel_id=1, source_target_pairs={{0,28},{4,0},{8,4},{12,8},{16,12},{20,16},{24,20},{28,24},{1,29},{... | collective-permute-start | bytes 393224 | tf_op jit(solution)/shard_map/ppermute | solution.py:371
  41.1 0.1 copy.7
  41.2 0.7 reshape.3.ranks_ref
  41.9 2.0 %collective-permute-done.6.refs_7_ = bf16[4,2,64,128]{3,2,1,0:T(8,128)(2,1)} collective-permute-done((bf16[4,2,64,128]{3,2,1,0:T(8,128)(2,1)}, bf16[4,2,64,128]{3,2,1,0:T(8,128)(2,1)}, u32[]{:S(2)}, u32[]{:S(2)}) %collective-permute-start.6) | collective-permute-done | bytes 131104 | tf_op jit(solution)/shard_map/ppermute | solution.py:371
  43.9 5.3 %coefficients.1 = (bf16[4,2,32,128]{3,2,1,0:T(8,128)(2,1)}, bf16[4,2,32,128]{3,2,1,0:T(8,128)(2,1)}, bf16[4,2,32,128]{3,2,1,0:T(8,128)(2,1)}, bf16[4,2,32,128]{3...) custom-call(s32[256]{0:T(256)} %reshape.3.ranks_ref, ...), custom_call_target="tpu_custom_call" | custom-call | flops 536870912 | bytes 4194304 | tf_op jit(solution)/shard_map/coefficients/pallas_call | solution.py:194
  49.2 0.1 collective-permute-start.7
  49.3 2.6 %stage.3 = (bf16[4,2,4,16,512]{4,3,2,1,0:T(8,128)(2,1)}, bf16[4,2,4,16,512]{4,3,2,1,0:T(8,128)(2,1)}, bf16[4,2,4,16,512]{4,3,2,1,0:T(8,128)(2,1)}) custom-call(bf16[4,16,4,16,512]{4,3,2,1,0:T(8,128)(2,1)} %refs_0_.3), custom_call_target="tpu_custom_call" | custom-call | flops 268435456 | bytes 4194304 | tf_op jit(solution)/shard_map/stage/pallas_call | solution.py:115
  51.9 0.5 collective-permute-start.20
  52.4 1.5 %collective-permute-start.21 = (bf16[4,2,4,16,512]{4,3,2,1,0:T(8,128)(2,1)}, bf16[4,2,4,16,512]{4,3,2,1,0:T(8,128)(2,1)S(1)}, u32[]{:S(2)}, u32[]{:S(2)}) collective-permute-start(bf16[4,2,4,16,512]{4,3,2,1,0:T(8,128)(2,1)} %get-tuple-element.65), channel_id=1, source_target_pairs={{0,2},{1,3},{2,0},{3,1},{4,6},{5,7},{6,4},{7,5},{8,10},{9,11},{10,... | collective-permute-start | bytes 1572872 | tf_op jit(solution)/shard_map/ppermute | solution.py:371
  53.9 1.0 collective-permute-start.22
  54.9 0.9 copy-done.1
  55.8 0.4 synthesis.3
  56.2 0.6 collective-permute-start.9
  56.8 32.4 %collective-permute-done.17.refs_1_ = bf16[4,2,32,128]{3,2,1,0:T(8,128)(2,1)S(1)} collective-permute-done((bf16[4,2,32,128]{3,2,1,0:T(8,128)(2,1)}, bf16[4,2,32,128]{3,2,1,0:T(8,128)(2,1)S(1)}, u32[]{:S(2)}, u32[]{:S(2)}) %collective-permute-start.17) | collective-permute-done | bytes 65568 | tf_op jit(solution)/shard_map/ppermute | solution.py:371
  89.2 1.5 %collective-permute-start.18 = (bf16[4,2,32,128]{3,2,1,0:T(8,128)(2,1)}, bf16[4,2,32,128]{3,2,1,0:T(8,128)(2,1)S(1)}, u32[]{:S(2)}, u32[]{:S(2)}) collective-permute-start(bf16[4,2,32,128]{3,2,1,0:T(8,128)(2,1)} %get-tuple-element.62), channel_id=1, source_target_pairs={{0,2},{1,3},{2,0},{3,1},{4,6},{5,7},{6,4},{7,5},{8,10},{9,11},{10,... | collective-permute-start | bytes 196616 | tf_op jit(solution)/shard_map/ppermute | solution.py:371
  90.7 3.0 %collective-permute-done.18.refs_2_ = bf16[4,2,32,128]{3,2,1,0:T(8,128)(2,1)S(1)} collective-permute-done((bf16[4,2,32,128]{3,2,1,0:T(8,128)(2,1)}, bf16[4,2,32,128]{3,2,1,0:T(8,128)(2,1)S(1)}, u32[]{:S(2)}, u32[]{:S(2)}) %collective-permute-start.18) | collective-permute-done | bytes 65568 | tf_op jit(solution)/shard_map/ppermute | solution.py:371
  93.6 2.2 %collective-permute-done.19.refs_3_ = bf16[4,2,32,128]{3,2,1,0:T(8,128)(2,1)S(1)} collective-permute-done((bf16[4,2,32,128]{3,2,1,0:T(8,128)(2,1)}, bf16[4,2,32,128]{3,2,1,0:T(8,128)(2,1)S(1)}, u32[]{:S(2)}, u32[]{:S(2)}) %collective-permute-start.19) | collective-permute-done | bytes 65568 | tf_op jit(solution)/shard_map/ppermute | solution.py:371
  95.9 0.8 copy-done.3
  96.7 0.8 synthesis.5
  97.6 3.4 %collective-permute-start.24 = (bf16[4,64,128]{2,1,0:T(8,128)(2,1)S(1)}, bf16[4,64,128]{2,1,0:T(8,128)(2,1)S(1)}, u32[]{:S(2)}, u32[]{:S(2)}) collective-permute-start(bf16[4,64,128]{2,1,0:T(8,128)(2,1)S(1)} %get-tuple-element.69), channel_id=1, source_target_pairs={{0,8},{4,12},{8,16},{12,20},{16,24},{20,28},{24,0},{28,4},{1,9},{5... | collective-permute-start | bytes 196616 | tf_op jit(solution)/shard_map/ppermute | solution.py:371
  101.0 3.3 %collective-permute-start.25 = (bf16[4,64,128]{2,1,0:T(8,128)(2,1)S(1)}, bf16[4,64,128]{2,1,0:T(8,128)(2,1)S(1)}, u32[]{:S(2)}, u32[]{:S(2)}) collective-permute-start(bf16[4,64,128]{2,1,0:T(8,128)(2,1)S(1)} %get-tuple-element.70), channel_id=1, source_target_pairs={{0,12},{4,16},{8,20},{12,24},{16,28},{20,0},{24,4},{28,8},{1,13},{... | collective-permute-start | bytes 196616 | tf_op jit(solution)/shard_map/ppermute | solution.py:371
  104.3 3.4 %collective-permute-start.27 = (bf16[4,64,128]{2,1,0:T(8,128)(2,1)S(1)}, bf16[4,64,128]{2,1,0:T(8,128)(2,1)S(1)}, u32[]{:S(2)}, u32[]{:S(2)}) collective-permute-start(bf16[4,64,128]{2,1,0:T(8,128)(2,1)S(1)} %get-tuple-element.72), channel_id=1, source_target_pairs={{0,20},{4,24},{8,28},{12,0},{16,4},{20,8},{24,12},{28,16},{1,21},{... | collective-permute-start | bytes 196616 | tf_op jit(solution)/shard_map/ppermute | solution.py:371
  107.7 0.5 synthesis.4
  108.2 1.4 %collective-permute-start.28 = (bf16[4,64,128]{2,1,0:T(8,128)(2,1)S(1)}, bf16[4,64,128]{2,1,0:T(8,128)(2,1)S(1)}, u32[]{:S(2)}, u32[]{:S(2)}) collective-permute-start(bf16[4,64,128]{2,1,0:T(8,128)(2,1)S(1)} %get-tuple-element.73), channel_id=1, source_target_pairs={{0,24},{4,28},{8,0},{12,4},{16,8},{20,12},{24,16},{28,20},{1,25},{... | collective-permute-start | bytes 196616 | tf_op jit(solution)/shard_map/ppermute | solution.py:371
  109.6 0.6 collective-permute-start.29
  110.3 1.0 collective-permute-done.25.refs_3_
  111.3 0.4 collective-permute-start.10
  111.7 0.9 collective-permute-done.26.refs_4_
  112.5 5.9 %collective-permute-start.12 = (bf16[4,64,128]{2,1,0:T(8,128)(2,1)S(1)}, bf16[4,64,128]{2,1,0:T(8,128)(2,1)S(1)}, u32[]{:S(2)}, u32[]{:S(2)}) collective-permute-start(bf16[4,64,128]{2,1,0:T(8,128)(2,1)S(1)} %get-tuple-element.55), channel_id=1, source_target_pairs={{0,12},{4,16},{8,20},{12,24},{16,28},{20,0},{24,4},{28,8},{1,13},{... | collective-permute-start | bytes 196616 | tf_op jit(solution)/shard_map/ppermute | solution.py:371
  118.4 1.2 collective-permute-start.13
  119.6 1.2 collective-permute-start.14
  120.8 1.5 %collective-permute-start.15 = (bf16[4,64,128]{2,1,0:T(8,128)(2,1)S(1)}, bf16[4,64,128]{2,1,0:T(8,128)(2,1)S(1)}, u32[]{:S(2)}, u32[]{:S(2)}) collective-permute-start(bf16[4,64,128]{2,1,0:T(8,128)(2,1)S(1)} %get-tuple-element.58), channel_id=1, source_target_pairs={{0,24},{4,28},{8,0},{12,4},{16,8},{20,12},{24,16},{28,20},{1,25},{... | collective-permute-start | bytes 196616 | tf_op jit(solution)/shard_map/ppermute | solution.py:371
  122.2 1.5 %collective-permute-start.16 = (bf16[4,64,128]{2,1,0:T(8,128)(2,1)S(1)}, bf16[4,64,128]{2,1,0:T(8,128)(2,1)S(1)}, u32[]{:S(2)}, u32[]{:S(2)}) collective-permute-start(bf16[4,64,128]{2,1,0:T(8,128)(2,1)S(1)} %get-tuple-element.59), channel_id=1, source_target_pairs={{0,28},{4,0},{8,4},{12,8},{16,12},{20,16},{24,20},{28,24},{1,29},{... | collective-permute-start | bytes 196616 | tf_op jit(solution)/shard_map/ppermute | solution.py:371
  123.8 4.4 %inverse.2.refs_8_ = bf16[4,64,64,512]{3,2,1,0:T(8,128)(2,1)} custom-call(bf16[32,512]{1,0:T(8,128)(2,1)S(1)} %copy-done.2, bf16[4,64,128]{2,1,0:T(8,128)(2,1)S(1)} %get-tuple-element.67.refs_0_, bf16[4,64,128]{2,1,0:T(8,128)(2,1)S(1)} %collective-permute-done.23.refs_1_, bf16[4,64,128]{2,1,0:T(8,128)(2,1)S(1)} %collective-permute-done.24.refs_2_, ...), custom_call_target="tpu_custom_call" | custom-call | flops 268435456 | bytes 8388608 | tf_op jit(solution)/shard_map/inverse/pallas_call | solution.py:337
  128.2 4.4 %inverse.3 = bf16[4,64,64,512]{3,2,1,0:T(8,128)(2,1)} custom-call(bf16[32,512]{1,0:T(8,128)(2,1)S(1)} %copy-done.2, bf16[4,64,128]{2,1,0:T(8,128)(2,1)S(1)} %get-tuple-element.52.refs_0_, bf16[4,64,128]{2,1,0:T(8,128)(2,1)S(1)} %collective-permute-done.10.refs_1_, ...), custom_call_target="tpu_custom_call", output_to_operand_aliasing={{}: (9, {})} | custom-call | flops 268435456 | bytes 8388608 | tf_op jit(solution)/shard_map/inverse/pallas_call | solution.py:337
  (45 shorter events, 0.2 us)
Async XLA Ops:
  0.0 2.2 %copy-start = (bf16[4,16,4,16,512]{4,3,2,1,0:T(8,128)(2,1)S(1)}, bf16[4,16,4,16,512]{4,3,2,1,0:T(8,128)(2,1)}, u32[]{:S(2)}) copy-start(bf16[4,16,4,16,512]{4,3,2,1,0:T(8,128)(2,1)} %refs_0_.3) | copy-start | bytes 12582916
  2.2 38.9 %copy-start.10 = (s32[4,16,4]{1,2,0:T(4,128)S(1)}, s32[4,16,4]{1,2,0:T(4,128)}, u32[]{:S(2)}) copy-start(s32[4,16,4]{1,2,0:T(4,128)} %param.8) | copy-start | bytes 3076
  3.4 120.4 %copy-start.2 = (bf16[32,512]{1,0:T(8,128)(2,1)S(1)}, bf16[32,512]{1,0:T(8,128)(2,1)}, u32[]{:S(2)}) copy-start(bf16[32,512]{1,0:T(8,128)(2,1)} %constant.2.clone.cas_ref) | copy-start | bytes 98308
  3.4 51.5 %collective-permute-start.8 = (bf16[4,2,2,4,16,512]{5,4,3,2,1,0:T(8,128)(2,1)}, bf16[4,2,2,4,16,512]{5,4,3,2,1,0:T(8,128)(2,1)S(1)}, u32[]{:S(2)}, u32[]{:S(2)}) collective-permute-start(bf16[4,2,2,4,16,512]{5,4,3,2,1,0:T(8,128)(2,1)} %get-tuple-element.51), channel_id=1, source_target_pairs={{0,1},{1,0},{2,3},{3,2},{4,5},{5,4},{6,7},{7,6},{8,9},{9,8},{10,11... | collective-permute-start | bytes 3145736 | tf_op jit(solution)/shard_map/ppermute | solution.py:381
  14.4 10.3 %collective-permute-start = (bf16[4,2,64,128]{3,2,1,0:T(8,128)(2,1)}, bf16[4,2,64,128]{3,2,1,0:T(8,128)(2,1)S(1)}, u32[]{:S(2)}, u32[]{:S(2)}) collective-permute-start(bf16[4,2,64,128]{3,2,1,0:T(8,128)(2,1)} %get-tuple-element.41), channel_id=1, source_target_pairs={{0,4},{4,8},{8,12},{12,16},{16,20},{20,24},{24,28},{28,0},{1,5},{5... | collective-permute-start | bytes 393224 | tf_op jit(solution)/shard_map/ppermute | solution.py:371
  17.0 8.4 %collective-permute-start.1 = (bf16[4,2,64,128]{3,2,1,0:T(8,128)(2,1)}, bf16[4,2,64,128]{3,2,1,0:T(8,128)(2,1)S(1)}, u32[]{:S(2)}, u32[]{:S(2)}) collective-permute-start(bf16[4,2,64,128]{3,2,1,0:T(8,128)(2,1)} %get-tuple-element.42), channel_id=1, source_target_pairs={{0,8},{4,12},{8,16},{12,20},{16,24},{20,28},{24,0},{28,4},{1,9},{5... | collective-permute-start | bytes 393224 | tf_op jit(solution)/shard_map/ppermute | solution.py:371
  18.6 17.2 %collective-permute-start.2 = (bf16[4,2,64,128]{3,2,1,0:T(8,128)(2,1)}, bf16[4,2,64,128]{3,2,1,0:T(8,128)(2,1)S(1)}, u32[]{:S(2)}, u32[]{:S(2)}) collective-permute-start(bf16[4,2,64,128]{3,2,1,0:T(8,128)(2,1)} %get-tuple-element.43), channel_id=1, source_target_pairs={{0,12},{4,16},{8,20},{12,24},{16,28},{20,0},{24,4},{28,8},{1,13},{... | collective-permute-start | bytes 393224 | tf_op jit(solution)/shard_map/ppermute | solution.py:371
  21.1 20.7 %collective-permute-start.3 = (bf16[4,2,64,128]{3,2,1,0:T(8,128)(2,1)}, bf16[4,2,64,128]{3,2,1,0:T(8,128)(2,1)S(1)}, u32[]{:S(2)}, u32[]{:S(2)}) collective-permute-start(bf16[4,2,64,128]{3,2,1,0:T(8,128)(2,1)} %get-tuple-element.44), channel_id=1, source_target_pairs={{0,16},{4,20},{8,24},{12,28},{16,0},{20,4},{24,8},{28,12},{1,17},{... | collective-permute-start | bytes 393224 | tf_op jit(solution)/shard_map/ppermute | solution.py:371
  24.7 19.2 %copy-start.4 = (bf16[4,2,64,128]{3,2,1,0:T(8,128)(2,1)}, bf16[4,2,64,128]{3,2,1,0:T(8,128)(2,1)S(1)}, u32[]{:S(2)}) copy-start(bf16[4,2,64,128]{3,2,1,0:T(8,128)(2,1)S(1)} %collective-permute-done.refs_1_) | copy-start | bytes 393220
  24.7 17.2 %collective-permute-start.4 = (bf16[4,2,64,128]{3,2,1,0:T(8,128)(2,1)}, bf16[4,2,64,128]{3,2,1,0:T(8,128)(2,1)S(1)}, u32[]{:S(2)}, u32[]{:S(2)}) collective-permute-start(bf16[4,2,64,128]{3,2,1,0:T(8,128)(2,1)} %get-tuple-element.45), channel_id=1, source_target_pairs={{0,20},{4,24},{8,28},{12,0},{16,4},{20,8},{24,12},{28,16},{1,21},{... | collective-permute-start | bytes 393224 | tf_op jit(solution)/shard_map/ppermute | solution.py:371
  25.4 18.5 %copy-start.5 = (bf16[4,2,64,128]{3,2,1,0:T(8,128)(2,1)}, bf16[4,2,64,128]{3,2,1,0:T(8,128)(2,1)S(1)}, u32[]{:S(2)}) copy-start(bf16[4,2,64,128]{3,2,1,0:T(8,128)(2,1)S(1)} %collective-permute-done.1.refs_2_) | copy-start | bytes 393220
  25.4 16.5 %collective-permute-start.5 = (bf16[4,2,64,128]{3,2,1,0:T(8,128)(2,1)}, bf16[4,2,64,128]{3,2,1,0:T(8,128)(2,1)S(1)}, u32[]{:S(2)}, u32[]{:S(2)}) collective-permute-start(bf16[4,2,64,128]{3,2,1,0:T(8,128)(2,1)} %get-tuple-element.46), channel_id=1, source_target_pairs={{0,24},{4,28},{8,0},{12,4},{16,8},{20,12},{24,16},{28,20},{1,25},{... | collective-permute-start | bytes 393224 | tf_op jit(solution)/shard_map/ppermute | solution.py:371
  35.7 8.2 %copy-start.6 = (bf16[4,2,64,128]{3,2,1,0:T(8,128)(2,1)}, bf16[4,2,64,128]{3,2,1,0:T(8,128)(2,1)S(1)}, u32[]{:S(2)}) copy-start(bf16[4,2,64,128]{3,2,1,0:T(8,128)(2,1)S(1)} %collective-permute-done.2.refs_3_) | copy-start | bytes 393220
  35.7 8.2 %collective-permute-start.6 = (bf16[4,2,64,128]{3,2,1,0:T(8,128)(2,1)}, bf16[4,2,64,128]{3,2,1,0:T(8,128)(2,1)}, u32[]{:S(2)}, u32[]{:S(2)}) collective-permute-start(bf16[4,2,64,128]{3,2,1,0:T(8,128)(2,1)} %get-tuple-element.47), channel_id=1, source_target_pairs={{0,28},{4,0},{8,4},{12,8},{16,12},{20,16},{24,20},{28,24},{1,29},{... | collective-permute-start | bytes 393224 | tf_op jit(solution)/shard_map/ppermute | solution.py:371
  41.9 2.1 %copy-start.7 = (bf16[4,2,64,128]{3,2,1,0:T(8,128)(2,1)}, bf16[4,2,64,128]{3,2,1,0:T(8,128)(2,1)S(1)}, u32[]{:S(2)}) copy-start(bf16[4,2,64,128]{3,2,1,0:T(8,128)(2,1)S(1)} %collective-permute-done.3.refs_4_) | copy-start | bytes 393220
  41.9 2.0 %copy-start.8 = (bf16[4,2,64,128]{3,2,1,0:T(8,128)(2,1)}, bf16[4,2,64,128]{3,2,1,0:T(8,128)(2,1)S(1)}, u32[]{:S(2)}) copy-start(bf16[4,2,64,128]{3,2,1,0:T(8,128)(2,1)S(1)} %collective-permute-done.4.refs_5_) | copy-start | bytes 393220
  41.9 2.0 %copy-start.9 = (bf16[4,2,64,128]{3,2,1,0:T(8,128)(2,1)}, bf16[4,2,64,128]{3,2,1,0:T(8,128)(2,1)S(1)}, u32[]{:S(2)}) copy-start(bf16[4,2,64,128]{3,2,1,0:T(8,128)(2,1)S(1)} %collective-permute-done.5.refs_6_) | copy-start | bytes 393220
  49.2 5.7 %collective-permute-start.7 = (bf16[4,2,2,32,128]{4,3,2,1,0:T(8,128)(2,1)}, bf16[4,2,2,32,128]{4,3,2,1,0:T(8,128)(2,1)S(1)}, u32[]{:S(2)}, u32[]{:S(2)}) collective-permute-start(bf16[4,2,2,32,128]{4,3,2,1,0:T(8,128)(2,1)} %get-tuple-element.49), channel_id=1, source_target_pairs={{0,1},{1,0},{2,3},{3,2},{4,5},{5,4},{6,7},{7,6},{8,9},{9,8},{10,11... | collective-permute-start | bytes 393224 | tf_op jit(solution)/shard_map/ppermute | solution.py:381
  51.9 44.0 %collective-permute-start.20 = (bf16[4,2,4,16,512]{4,3,2,1,0:T(8,128)(2,1)}, bf16[4,2,4,16,512]{4,3,2,1,0:T(8,128)(2,1)S(1)}, u32[]{:S(2)}, u32[]{:S(2)}) collective-permute-start(bf16[4,2,4,16,512]{4,3,2,1,0:T(8,128)(2,1)} %get-tuple-element.64), channel_id=1, source_target_pairs={{0,1},{1,2},{2,3},{3,0},{4,5},{5,6},{6,7},{7,4},{8,9},{9,10},{10,1... | collective-permute-start | bytes 1572872 | tf_op jit(solution)/shard_map/ppermute | solution.py:371
  52.4 43.5 %collective-permute-start.21 = (bf16[4,2,4,16,512]{4,3,2,1,0:T(8,128)(2,1)}, bf16[4,2,4,16,512]{4,3,2,1,0:T(8,128)(2,1)S(1)}, u32[]{:S(2)}, u32[]{:S(2)}) collective-permute-start(bf16[4,2,4,16,512]{4,3,2,1,0:T(8,128)(2,1)} %get-tuple-element.65), channel_id=1, source_target_pairs={{0,2},{1,3},{2,0},{3,1},{4,6},{5,7},{6,4},{7,5},{8,10},{9,11},{10,... | collective-permute-start | bytes 1572872 | tf_op jit(solution)/shard_map/ppermute | solution.py:371
  53.9 42.0 %collective-permute-start.22 = (bf16[4,2,4,16,512]{4,3,2,1,0:T(8,128)(2,1)}, bf16[4,2,4,16,512]{4,3,2,1,0:T(8,128)(2,1)S(1)}, u32[]{:S(2)}, u32[]{:S(2)}) collective-permute-start(bf16[4,2,4,16,512]{4,3,2,1,0:T(8,128)(2,1)} %get-tuple-element.66), channel_id=1, source_target_pairs={{0,3},{1,0},{2,1},{3,2},{4,7},{5,4},{6,5},{7,6},{8,11},{9,8},{10,9... | collective-permute-start | bytes 1572872 | tf_op jit(solution)/shard_map/ppermute | solution.py:371
  54.9 0.9 copy-start.1
  56.2 48.1 %collective-permute-start.9 = (bf16[4,2,64,512]{3,2,1,0:T(8,128)(2,1)S(1)}, bf16[4,2,64,512]{3,2,1,0:T(8,128)(2,1)S(1)}, u32[]{:S(2)}, u32[]{:S(2)}) collective-permute-start(bf16[4,2,64,512]{3,2,1,0:T(8,128)(2,1)S(1)} %synthesis.3), channel_id=1, source_target_pairs={{0,2},{1,3},{2,0},{3,1},{4,6},{5,7},{6,4},{7,5},{8,10},{9,11},{10,... | collective-permute-start | bytes 1572872 | tf_op jit(solution)/shard_map/ppermute | solution.py:381
  56.8 32.4 %collective-permute-start.17 = (bf16[4,2,32,128]{3,2,1,0:T(8,128)(2,1)}, bf16[4,2,32,128]{3,2,1,0:T(8,128)(2,1)S(1)}, u32[]{:S(2)}, u32[]{:S(2)}) collective-permute-start(bf16[4,2,32,128]{3,2,1,0:T(8,128)(2,1)} %get-tuple-element.61), channel_id=1, source_target_pairs={{0,1},{1,2},{2,3},{3,0},{4,5},{5,6},{6,7},{7,4},{8,9},{9,10},{10,1... | collective-permute-start | bytes 196616 | tf_op jit(solution)/shard_map/ppermute | solution.py:371
  89.2 4.5 %collective-permute-start.18 = (bf16[4,2,32,128]{3,2,1,0:T(8,128)(2,1)}, bf16[4,2,32,128]{3,2,1,0:T(8,128)(2,1)S(1)}, u32[]{:S(2)}, u32[]{:S(2)}) collective-permute-start(bf16[4,2,32,128]{3,2,1,0:T(8,128)(2,1)} %get-tuple-element.62), channel_id=1, source_target_pairs={{0,2},{1,3},{2,0},{3,1},{4,6},{5,7},{6,4},{7,5},{8,10},{9,11},{10,... | collective-permute-start | bytes 196616 | tf_op jit(solution)/shard_map/ppermute | solution.py:371
  93.6 2.2 %collective-permute-start.19 = (bf16[4,2,32,128]{3,2,1,0:T(8,128)(2,1)}, bf16[4,2,32,128]{3,2,1,0:T(8,128)(2,1)S(1)}, u32[]{:S(2)}, u32[]{:S(2)}) collective-permute-start(bf16[4,2,32,128]{3,2,1,0:T(8,128)(2,1)} %get-tuple-element.63), channel_id=1, source_target_pairs={{0,3},{1,0},{2,1},{3,2},{4,7},{5,4},{6,5},{7,6},{8,11},{9,8},{10,9... | collective-permute-start | bytes 196616 | tf_op jit(solution)/shard_map/ppermute | solution.py:371
  95.9 0.8 copy-start.3
  97.5 10.7 %collective-permute-start.23 = (bf16[4,64,128]{2,1,0:T(8,128)(2,1)S(1)}, bf16[4,64,128]{2,1,0:T(8,128)(2,1)S(1)}, u32[]{:S(2)}, u32[]{:S(2)}) collective-permute-start(bf16[4,64,128]{2,1,0:T(8,128)(2,1)S(1)} %get-tuple-element.68), channel_id=1, source_target_pairs={{0,4},{4,8},{8,12},{12,16},{16,20},{20,24},{24,28},{28,0},{1,5},{5... | collective-permute-start | bytes 196616 | tf_op jit(solution)/shard_map/ppermute | solution.py:371
  97.6 12.0 %collective-permute-start.24 = (bf16[4,64,128]{2,1,0:T(8,128)(2,1)S(1)}, bf16[4,64,128]{2,1,0:T(8,128)(2,1)S(1)}, u32[]{:S(2)}, u32[]{:S(2)}) collective-permute-start(bf16[4,64,128]{2,1,0:T(8,128)(2,1)S(1)} %get-tuple-element.69), channel_id=1, source_target_pairs={{0,8},{4,12},{8,16},{12,20},{16,24},{20,28},{24,0},{28,4},{1,9},{5... | collective-permute-start | bytes 196616 | tf_op jit(solution)/shard_map/ppermute | solution.py:371
  101.0 10.3 %collective-permute-start.25 = (bf16[4,64,128]{2,1,0:T(8,128)(2,1)S(1)}, bf16[4,64,128]{2,1,0:T(8,128)(2,1)S(1)}, u32[]{:S(2)}, u32[]{:S(2)}) collective-permute-start(bf16[4,64,128]{2,1,0:T(8,128)(2,1)S(1)} %get-tuple-element.70), channel_id=1, source_target_pairs={{0,12},{4,16},{8,20},{12,24},{16,28},{20,0},{24,4},{28,8},{1,13},{... | collective-permute-start | bytes 196616 | tf_op jit(solution)/shard_map/ppermute | solution.py:371
  104.3 8.2 %collective-permute-start.26 = (bf16[4,64,128]{2,1,0:T(8,128)(2,1)S(1)}, bf16[4,64,128]{2,1,0:T(8,128)(2,1)S(1)}, u32[]{:S(2)}, u32[]{:S(2)}) collective-permute-start(bf16[4,64,128]{2,1,0:T(8,128)(2,1)S(1)} %get-tuple-element.71), channel_id=1, source_target_pairs={{0,16},{4,20},{8,24},{12,28},{16,0},{20,4},{24,8},{28,12},{1,17},{... | collective-permute-start | bytes 196616 | tf_op jit(solution)/shard_map/ppermute | solution.py:371
  104.3 8.2 %collective-permute-start.27 = (bf16[4,64,128]{2,1,0:T(8,128)(2,1)S(1)}, bf16[4,64,128]{2,1,0:T(8,128)(2,1)S(1)}, u32[]{:S(2)}, u32[]{:S(2)}) collective-permute-start(bf16[4,64,128]{2,1,0:T(8,128)(2,1)S(1)} %get-tuple-element.72), channel_id=1, source_target_pairs={{0,20},{4,24},{8,28},{12,0},{16,4},{20,8},{24,12},{28,16},{1,21},{... | collective-permute-start | bytes 196616 | tf_op jit(solution)/shard_map/ppermute | solution.py:371
  108.2 10.2 %collective-permute-start.28 = (bf16[4,64,128]{2,1,0:T(8,128)(2,1)S(1)}, bf16[4,64,128]{2,1,0:T(8,128)(2,1)S(1)}, u32[]{:S(2)}, u32[]{:S(2)}) collective-permute-start(bf16[4,64,128]{2,1,0:T(8,128)(2,1)S(1)} %get-tuple-element.73), channel_id=1, source_target_pairs={{0,24},{4,28},{8,0},{12,4},{16,8},{20,12},{24,16},{28,20},{1,25},{... | collective-permute-start | bytes 196616 | tf_op jit(solution)/shard_map/ppermute | solution.py:371
  109.6 10.0 %collective-permute-start.29 = (bf16[4,64,128]{2,1,0:T(8,128)(2,1)S(1)}, bf16[4,64,128]{2,1,0:T(8,128)(2,1)S(1)}, u32[]{:S(2)}, u32[]{:S(2)}) collective-permute-start(bf16[4,64,128]{2,1,0:T(8,128)(2,1)S(1)} %get-tuple-element.74), channel_id=1, source_target_pairs={{0,28},{4,0},{8,4},{12,8},{16,12},{20,16},{24,20},{28,24},{1,29},{... | collective-permute-start | bytes 196616 | tf_op jit(solution)/shard_map/ppermute | solution.py:371
  111.3 9.5 %collective-permute-start.10 = (bf16[4,64,128]{2,1,0:T(8,128)(2,1)S(1)}, bf16[4,64,128]{2,1,0:T(8,128)(2,1)S(1)}, u32[]{:S(2)}, u32[]{:S(2)}) collective-permute-start(bf16[4,64,128]{2,1,0:T(8,128)(2,1)S(1)} %get-tuple-element.53), channel_id=1, source_target_pairs={{0,4},{4,8},{8,12},{12,16},{16,20},{20,24},{24,28},{28,0},{1,5},{5... | collective-permute-start | bytes 196616 | tf_op jit(solution)/shard_map/ppermute | solution.py:371
  112.5 9.7 %collective-permute-start.11 = (bf16[4,64,128]{2,1,0:T(8,128)(2,1)S(1)}, bf16[4,64,128]{2,1,0:T(8,128)(2,1)S(1)}, u32[]{:S(2)}, u32[]{:S(2)}) collective-permute-start(bf16[4,64,128]{2,1,0:T(8,128)(2,1)S(1)} %get-tuple-element.54), channel_id=1, source_target_pairs={{0,8},{4,12},{8,16},{12,20},{16,24},{20,28},{24,0},{28,4},{1,9},{5... | collective-permute-start | bytes 196616 | tf_op jit(solution)/shard_map/ppermute | solution.py:371
  112.5 15.6 %collective-permute-start.12 = (bf16[4,64,128]{2,1,0:T(8,128)(2,1)S(1)}, bf16[4,64,128]{2,1,0:T(8,128)(2,1)S(1)}, u32[]{:S(2)}, u32[]{:S(2)}) collective-permute-start(bf16[4,64,128]{2,1,0:T(8,128)(2,1)S(1)} %get-tuple-element.55), channel_id=1, source_target_pairs={{0,12},{4,16},{8,20},{12,24},{16,28},{20,0},{24,4},{28,8},{1,13},{... | collective-permute-start | bytes 196616 | tf_op jit(solution)/shard_map/ppermute | solution.py:371
  118.4 9.8 %collective-permute-start.13 = (bf16[4,64,128]{2,1,0:T(8,128)(2,1)S(1)}, bf16[4,64,128]{2,1,0:T(8,128)(2,1)S(1)}, u32[]{:S(2)}, u32[]{:S(2)}) collective-permute-start(bf16[4,64,128]{2,1,0:T(8,128)(2,1)S(1)} %get-tuple-element.56), channel_id=1, source_target_pairs={{0,16},{4,20},{8,24},{12,28},{16,0},{20,4},{24,8},{28,12},{1,17},{... | collective-permute-start | bytes 196616 | tf_op jit(solution)/shard_map/ppermute | solution.py:371
  119.6 8.6 %collective-permute-start.14 = (bf16[4,64,128]{2,1,0:T(8,128)(2,1)S(1)}, bf16[4,64,128]{2,1,0:T(8,128)(2,1)S(1)}, u32[]{:S(2)}, u32[]{:S(2)}) collective-permute-start(bf16[4,64,128]{2,1,0:T(8,128)(2,1)S(1)} %get-tuple-element.57), channel_id=1, source_target_pairs={{0,20},{4,24},{8,28},{12,0},{16,4},{20,8},{24,12},{28,16},{1,21},{... | collective-permute-start | bytes 196616 | tf_op jit(solution)/shard_map/ppermute | solution.py:371
  120.8 7.5 %collective-permute-start.15 = (bf16[4,64,128]{2,1,0:T(8,128)(2,1)S(1)}, bf16[4,64,128]{2,1,0:T(8,128)(2,1)S(1)}, u32[]{:S(2)}, u32[]{:S(2)}) collective-permute-start(bf16[4,64,128]{2,1,0:T(8,128)(2,1)S(1)} %get-tuple-element.58), channel_id=1, source_target_pairs={{0,24},{4,28},{8,0},{12,4},{16,8},{20,12},{24,16},{28,20},{1,25},{... | collective-permute-start | bytes 196616 | tf_op jit(solution)/shard_map/ppermute | solution.py:371
  122.2 6.0 %collective-permute-start.16 = (bf16[4,64,128]{2,1,0:T(8,128)(2,1)S(1)}, bf16[4,64,128]{2,1,0:T(8,128)(2,1)S(1)}, u32[]{:S(2)}, u32[]{:S(2)}) collective-permute-start(bf16[4,64,128]{2,1,0:T(8,128)(2,1)S(1)} %get-tuple-element.59), channel_id=1, source_target_pairs={{0,28},{4,0},{8,4},{12,8},{16,12},{20,16},{24,20},{28,24},{1,29},{... | collective-permute-start | bytes 196616 | tf_op jit(solution)/shard_map/ppermute | solution.py:371

commit v2 on v1

--- a/solution.py
+++ b/solution.py
@@ -126,13 +126,17 @@
 
 def coeff_kernel(ranks_ref, right_ref, *refs, shares, owners, inner):
     spectra, direct = refs[:shares], refs[shares : shares + owners]
-    paired, (spec_ref, rows_ref, right_held, own_held, arrived) = refs[shares + owners : -5], refs[-5:]
+    paired, (spec_ref, rows_ref, right_held, spec_held, arrived) = refs[shares + owners : -5], refs[-5:]
     freqs, receivers, tiles, ranks, sources = right_ref.shape
-    own = pltpu.make_async_copy(spectra[0], own_held, arrived.at[freqs])
-    own.start()
+    moves = [
+        pltpu.make_async_copy(spectra[shift], spec_held.at[shift], arrived.at[freqs + shift])
+        for shift in range(shares)
+    ]
     for k in range(freqs):
         pltpu.make_async_copy(right_ref.at[k], right_held.at[k], arrived.at[k]).start()
-    spectra = [own_held] + list(spectra[1:])
+        if k == 0:
+            for move in moves:
+                move.start()
     pairs, each = spectra[0].shape[1:3]
     pack = tiles // pairs
     waves = LANES // pack
@@ -141,14 +145,15 @@
     rank_row = lax.broadcasted_iota(jnp.int32, (ranks, LANES), 0)
     per_owner = receivers // owners
 
-    own.wait()
+    for move in moves:
+        move.wait()
 
     def body(k, carry):
         pltpu.make_async_copy(right_ref.at[k], right_held.at[k], arrived.at[k]).wait()
         for pair in range(pairs):
             for shift in range(shares):
                 first = pl.multiple_of(lax.rem(place + shares - shift, shares) * each, each)
-                spec_ref[pair, pl.ds(first, each), :] = spectra[shift][k, pair]
+                spec_ref[pair, pl.ds(first, each), :] = spec_held[shift, k, pair]
         for pair in range(pairs):
             product = [
                 jnp.dot(
@@ -195,14 +200,14 @@
         functools.partial(coeff_kernel, shares=shares, owners=owners, inner=inner),
         out_shape=[jax.ShapeDtypeStruct((freqs, pairs, rows, LANES), jnp.bfloat16)] * owners
         + [jax.ShapeDtypeStruct((freqs, outer, pairs, rows, LANES), jnp.bfloat16)] * inner,
-        in_specs=[smem, anywhere, anywhere] + [vmem] * (shares - 1),
+        in_specs=[smem, anywhere] + [anywhere] * shares,
         out_specs=[vmem] * (owners + inner),
         scratch_shapes=[
             pltpu.VMEM((pairs, sources, LANES), jnp.bfloat16),
             pltpu.VMEM((pairs, receivers, rank_count, LANES), jnp.bfloat16),
             pltpu.VMEM(right.shape, jnp.bfloat16),
-            pltpu.VMEM(spectra[0].shape, jnp.bfloat16),
-            pltpu.SemaphoreType.DMA((freqs + 1,)),
+            pltpu.VMEM((shares,) + spectra[0].shape, jnp.bfloat16),
+            pltpu.SemaphoreType.DMA((freqs + shares,)),
         ],
         cost_estimate=pl.CostEstimate(
             flops=2 * right.size * LANES, bytes_accessed=2 * right.size, transcendentals=0

time: 133 us -> 133 us (level)
  no operation moved by 1% of the time
where the time goes in v2:
time: 133 us; the launch traced here: 132 us
  waiting for transfers between devices  52.7 us (40%)
  starting transfers between devices  44.9 us (34%)
  Pallas kernels  29.8 us (22%)
  local copies, waits for them, and re-layouts  4.75 us (4%)
    ppermute x27, waiting for transfers between devices, shifted(): lax.ppermute(block, axis, [(i, (i + shift) % size) for i in range(size)])  52.7 us
    ppermute x27, starting transfers between devices, shifted(): lax.ppermute(block, axis, [(i, (i + shift) % size) for i in range(size)])  43.7 us
    pallas_call x1, Pallas kernels, forward(): pl.pallas_call(functools.partial(forward_kernel, shares=shares, depth=4,...  10.4 us
    pallas_call x2, Pallas kernels, inverse(): pl.pallas_call(functools.partial(inverse_kernel, shares=shares, group=gro...  8.87 us
    pallas_call x1, Pallas kernels, coefficients(): pl.pallas_call(functools.partial(coeff_kernel, shares=shares, owners=owne...  4.99 us
    unnamed x23, local copies, waits for them, and re-layouts  4.06 us
    pallas_call x2, Pallas kernels, stage(): pl.pallas_call(functools.partial(stage_kernel, count=len(operands), piece...  3.76 us
  transfers between devices with their start and end apart: 30, of which 9 were waited for; matrix products, arithmetic and copies ran while one was open for 1% of the time, Pallas kernels for 18%

profile of v2, /device:TPU:0, one launch (start us, length us, event | category | flops | bytes accessed | tf_op | source)
XLA Modules:
  0.0 132.4 jit_solution(18113771507848681343)
XLA Ops:
  0.0 2.2 %copy-done = bf16[4,16,4,16,512]{4,3,2,1,0:T(8,128)(2,1)S(1)} copy-done((bf16[4,16,4,16,512]{4,3,2,1,0:T(8,128)(2,1)S(1)}, bf16[4,16,4,16,512]{4,3,2,1,0:T(8,128)(2,1)}, u32[]{:S(2)}) %copy-start) | copy-done | bytes 4194328
  2.2 1.2 stage.2
  3.4 0.6 collective-permute-start.8
  4.0 10.4 %forward.1 = (bf16[4,2,64,128]{3,2,1,0:T(8,128)(2,1)}, bf16[4,2,64,128]{3,2,1,0:T(8,128)(2,1)}, bf16[4,2,64,128]{3,2,1,0:T(8,128)(2,1)}, bf16[4,2,64,128]{3,2,1,...) custom-call(bf16[4,64,64,512]{3,2,1,0:T(8,128)(2,1)} %x_ref.1, ...), custom_call_target="tpu_custom_call" | custom-call | flops 536870912 | bytes 16777216 | tf_op jit(solution)/shard_map/forward/pallas_call | solution.py:80
  14.4 2.6 %collective-permute-start = (bf16[4,2,64,128]{3,2,1,0:T(8,128)(2,1)}, bf16[4,2,64,128]{3,2,1,0:T(8,128)(2,1)S(1)}, u32[]{:S(2)}, u32[]{:S(2)}) collective-permute-start(bf16[4,2,64,128]{3,2,1,0:T(8,128)(2,1)} %get-tuple-element.41), channel_id=1, source_target_pairs={{0,4},{4,8},{8,12},{12,16},{16,20},{20,24},{24,28},{28,0},{1,5},{5... | collective-permute-start | bytes 393224 | tf_op jit(solution)/shard_map/ppermute | solution.py:376
  17.0 1.6 %collective-permute-start.1 = (bf16[4,2,64,128]{3,2,1,0:T(8,128)(2,1)}, bf16[4,2,64,128]{3,2,1,0:T(8,128)(2,1)S(1)}, u32[]{:S(2)}, u32[]{:S(2)}) collective-permute-start(bf16[4,2,64,128]{3,2,1,0:T(8,128)(2,1)} %get-tuple-element.42), channel_id=1, source_target_pairs={{0,8},{4,12},{8,16},{12,20},{16,24},{20,28},{24,0},{28,4},{1,9},{5... | collective-permute-start | bytes 393224 | tf_op jit(solution)/shard_map/ppermute | solution.py:376
  18.6 2.5 %collective-permute-start.2 = (bf16[4,2,64,128]{3,2,1,0:T(8,128)(2,1)}, bf16[4,2,64,128]{3,2,1,0:T(8,128)(2,1)S(1)}, u32[]{:S(2)}, u32[]{:S(2)}) collective-permute-start(bf16[4,2,64,128]{3,2,1,0:T(8,128)(2,1)} %get-tuple-element.43), channel_id=1, source_target_pairs={{0,12},{4,16},{8,20},{12,24},{16,28},{20,0},{24,4},{28,8},{1,13},{... | collective-permute-start | bytes 393224 | tf_op jit(solution)/shard_map/ppermute | solution.py:376
  21.1 1.2 collective-permute-start.3
  22.3 2.4 %collective-permute-done.refs_1_ = bf16[4,2,64,128]{3,2,1,0:T(8,128)(2,1)S(1)} collective-permute-done((bf16[4,2,64,128]{3,2,1,0:T(8,128)(2,1)}, bf16[4,2,64,128]{3,2,1,0:T(8,128)(2,1)S(1)}, u32[]{:S(2)}, u32[]{:S(2)}) %collective-permute-start) | collective-permute-done | bytes 131104 | tf_op jit(solution)/shard_map/ppermute | solution.py:376
  24.7 0.4 collective-permute-start.4
  25.1 0.3 collective-permute-done.1.refs_2_
  25.4 1.8 %collective-permute-start.5 = (bf16[4,2,64,128]{3,2,1,0:T(8,128)(2,1)}, bf16[4,2,64,128]{3,2,1,0:T(8,128)(2,1)S(1)}, u32[]{:S(2)}, u32[]{:S(2)}) collective-permute-start(bf16[4,2,64,128]{3,2,1,0:T(8,128)(2,1)} %get-tuple-element.46), channel_id=1, source_target_pairs={{0,24},{4,28},{8,0},{12,4},{16,8},{20,12},{24,16},{28,20},{1,25},{... | collective-permute-start | bytes 393224 | tf_op jit(solution)/shard_map/ppermute | solution.py:376
  27.2 8.5 %collective-permute-done.2.refs_3_ = bf16[4,2,64,128]{3,2,1,0:T(8,128)(2,1)S(1)} collective-permute-done((bf16[4,2,64,128]{3,2,1,0:T(8,128)(2,1)}, bf16[4,2,64,128]{3,2,1,0:T(8,128)(2,1)S(1)}, u32[]{:S(2)}, u32[]{:S(2)}) %collective-permute-start.2) | collective-permute-done | bytes 131104 | tf_op jit(solution)/shard_map/ppermute | solution.py:376
  35.7 5.3 %collective-permute-start.6 = (bf16[4,2,64,128]{3,2,1,0:T(8,128)(2,1)}, bf16[4,2,64,128]{3,2,1,0:T(8,128)(2,1)}, u32[]{:S(2)}, u32[]{:S(2)}) collective-permute-start(bf16[4,2,64,128]{3,2,1,0:T(8,128)(2,1)} %get-tuple-element.47), channel_id=1, source_target_pairs={{0,28},{4,0},{8,4},{12,8},{16,12},{20,16},{24,20},{28,24},{1,29},{... | collective-permute-start | bytes 393224 | tf_op jit(solution)/shard_map/ppermute | solution.py:376
  41.1 0.1 copy.7
  41.2 0.7 reshape.3.ranks_ref
  41.9 2.0 %collective-permute-done.6.refs_7_ = bf16[4,2,64,128]{3,2,1,0:T(8,128)(2,1)} collective-permute-done((bf16[4,2,64,128]{3,2,1,0:T(8,128)(2,1)}, bf16[4,2,64,128]{3,2,1,0:T(8,128)(2,1)}, u32[]{:S(2)}, u32[]{:S(2)}) %collective-permute-start.6) | collective-permute-done | bytes 131104 | tf_op jit(solution)/shard_map/ppermute | solution.py:376
  43.9 5.0 %coefficients.1 = (bf16[4,2,32,128]{3,2,1,0:T(8,128)(2,1)}, bf16[4,2,32,128]{3,2,1,0:T(8,128)(2,1)}, bf16[4,2,32,128]{3,2,1,0:T(8,128)(2,1)}, bf16[4,2,32,128]{3...) custom-call(s32[256]{0:T(256)} %reshape.3.ranks_ref, ...), custom_call_target="tpu_custom_call" | custom-call | flops 536870912 | bytes 4194304 | tf_op jit(solution)/shard_map/coefficients/pallas_call | solution.py:199
  48.9 0.1 collective-permute-start.7
  49.0 2.6 %stage.3 = (bf16[4,2,4,16,512]{4,3,2,1,0:T(8,128)(2,1)}, bf16[4,2,4,16,512]{4,3,2,1,0:T(8,128)(2,1)}, bf16[4,2,4,16,512]{4,3,2,1,0:T(8,128)(2,1)}) custom-call(bf16[4,16,4,16,512]{4,3,2,1,0:T(8,128)(2,1)} %refs_0_.3), custom_call_target="tpu_custom_call" | custom-call | flops 268435456 | bytes 4194304 | tf_op jit(solution)/shard_map/stage/pallas_call | solution.py:115
  51.6 0.5 collective-permute-start.20
  52.1 1.5 %collective-permute-start.21 = (bf16[4,2,4,16,512]{4,3,2,1,0:T(8,128)(2,1)}, bf16[4,2,4,16,512]{4,3,2,1,0:T(8,128)(2,1)S(1)}, u32[]{:S(2)}, u32[]{:S(2)}) collective-permute-start(bf16[4,2,4,16,512]{4,3,2,1,0:T(8,128)(2,1)} %get-tuple-element.65), channel_id=1, source_target_pairs={{0,2},{1,3},{2,0},{3,1},{4,6},{5,7},{6,4},{7,5},{8,10},{9,11},{10,... | collective-permute-start | bytes 1572872 | tf_op jit(solution)/shard_map/ppermute | solution.py:376
  53.6 1.0 collective-permute-start.22
  54.6 0.9 copy-done.1
  55.5 0.4 synthesis.3
  55.9 0.6 collective-permute-start.9
  56.5 32.4 %collective-permute-done.17.refs_1_ = bf16[4,2,32,128]{3,2,1,0:T(8,128)(2,1)S(1)} collective-permute-done((bf16[4,2,32,128]{3,2,1,0:T(8,128)(2,1)}, bf16[4,2,32,128]{3,2,1,0:T(8,128)(2,1)S(1)}, u32[]{:S(2)}, u32[]{:S(2)}) %collective-permute-start.17) | collective-permute-done | bytes 65568 | tf_op jit(solution)/shard_map/ppermute | solution.py:376
  88.9 1.5 %collective-permute-start.18 = (bf16[4,2,32,128]{3,2,1,0:T(8,128)(2,1)}, bf16[4,2,32,128]{3,2,1,0:T(8,128)(2,1)S(1)}, u32[]{:S(2)}, u32[]{:S(2)}) collective-permute-start(bf16[4,2,32,128]{3,2,1,0:T(8,128)(2,1)} %get-tuple-element.62), channel_id=1, source_target_pairs={{0,2},{1,3},{2,0},{3,1},{4,6},{5,7},{6,4},{7,5},{8,10},{9,11},{10,... | collective-permute-start | bytes 196616 | tf_op jit(solution)/shard_map/ppermute | solution.py:376
  90.4 3.0 %collective-permute-done.18.refs_2_ = bf16[4,2,32,128]{3,2,1,0:T(8,128)(2,1)S(1)} collective-permute-done((bf16[4,2,32,128]{3,2,1,0:T(8,128)(2,1)}, bf16[4,2,32,128]{3,2,1,0:T(8,128)(2,1)S(1)}, u32[]{:S(2)}, u32[]{:S(2)}) %collective-permute-start.18) | collective-permute-done | bytes 65568 | tf_op jit(solution)/shard_map/ppermute | solution.py:376
  93.4 2.2 %collective-permute-done.19.refs_3_ = bf16[4,2,32,128]{3,2,1,0:T(8,128)(2,1)S(1)} collective-permute-done((bf16[4,2,32,128]{3,2,1,0:T(8,128)(2,1)}, bf16[4,2,32,128]{3,2,1,0:T(8,128)(2,1)S(1)}, u32[]{:S(2)}, u32[]{:S(2)}) %collective-permute-start.19) | collective-permute-done | bytes 65568 | tf_op jit(solution)/shard_map/ppermute | solution.py:376
  95.6 0.8 copy-done.3
  96.4 0.8 synthesis.5
  97.3 3.4 %collective-permute-start.24 = (bf16[4,64,128]{2,1,0:T(8,128)(2,1)S(1)}, bf16[4,64,128]{2,1,0:T(8,128)(2,1)S(1)}, u32[]{:S(2)}, u32[]{:S(2)}) collective-permute-start(bf16[4,64,128]{2,1,0:T(8,128)(2,1)S(1)} %get-tuple-element.69), channel_id=1, source_target_pairs={{0,8},{4,12},{8,16},{12,20},{16,24},{20,28},{24,0},{28,4},{1,9},{5... | collective-permute-start | bytes 196616 | tf_op jit(solution)/shard_map/ppermute | solution.py:376
  100.7 3.3 %collective-permute-start.25 = (bf16[4,64,128]{2,1,0:T(8,128)(2,1)S(1)}, bf16[4,64,128]{2,1,0:T(8,128)(2,1)S(1)}, u32[]{:S(2)}, u32[]{:S(2)}) collective-permute-start(bf16[4,64,128]{2,1,0:T(8,128)(2,1)S(1)} %get-tuple-element.70), channel_id=1, source_target_pairs={{0,12},{4,16},{8,20},{12,24},{16,28},{20,0},{24,4},{28,8},{1,13},{... | collective-permute-start | bytes 196616 | tf_op jit(solution)/shard_map/ppermute | solution.py:376
  104.0 3.4 %collective-permute-start.27 = (bf16[4,64,128]{2,1,0:T(8,128)(2,1)S(1)}, bf16[4,64,128]{2,1,0:T(8,128)(2,1)S(1)}, u32[]{:S(2)}, u32[]{:S(2)}) collective-permute-start(bf16[4,64,128]{2,1,0:T(8,128)(2,1)S(1)} %get-tuple-element.72), channel_id=1, source_target_pairs={{0,20},{4,24},{8,28},{12,0},{16,4},{20,8},{24,12},{28,16},{1,21},{... | collective-permute-start | bytes 196616 | tf_op jit(solution)/shard_map/ppermute | solution.py:376
  107.4 0.5 synthesis.4
  107.9 1.4 %collective-permute-start.28 = (bf16[4,64,128]{2,1,0:T(8,128)(2,1)S(1)}, bf16[4,64,128]{2,1,0:T(8,128)(2,1)S(1)}, u32[]{:S(2)}, u32[]{:S(2)}) collective-permute-start(bf16[4,64,128]{2,1,0:T(8,128)(2,1)S(1)} %get-tuple-element.73), channel_id=1, source_target_pairs={{0,24},{4,28},{8,0},{12,4},{16,8},{20,12},{24,16},{28,20},{1,25},{... | collective-permute-start | bytes 196616 | tf_op jit(solution)/shard_map/ppermute | solution.py:376
  109.3 0.6 collective-permute-start.29
  110.0 1.0 collective-permute-done.25.refs_3_
  111.0 0.3 collective-permute-start.10
  111.4 0.9 collective-permute-done.26.refs_4_
  112.2 5.8 %collective-permute-start.12 = (bf16[4,64,128]{2,1,0:T(8,128)(2,1)S(1)}, bf16[4,64,128]{2,1,0:T(8,128)(2,1)S(1)}, u32[]{:S(2)}, u32[]{:S(2)}) collective-permute-start(bf16[4,64,128]{2,1,0:T(8,128)(2,1)S(1)} %get-tuple-element.55), channel_id=1, source_target_pairs={{0,12},{4,16},{8,20},{12,24},{16,28},{20,0},{24,4},{28,8},{1,13},{... | collective-permute-start | bytes 196616 | tf_op jit(solution)/shard_map/ppermute | solution.py:376
  118.1 1.2 collective-permute-start.13
  119.3 1.2 collective-permute-start.14
  120.5 1.5 %collective-permute-start.15 = (bf16[4,64,128]{2,1,0:T(8,128)(2,1)S(1)}, bf16[4,64,128]{2,1,0:T(8,128)(2,1)S(1)}, u32[]{:S(2)}, u32[]{:S(2)}) collective-permute-start(bf16[4,64,128]{2,1,0:T(8,128)(2,1)S(1)} %get-tuple-element.58), channel_id=1, source_target_pairs={{0,24},{4,28},{8,0},{12,4},{16,8},{20,12},{24,16},{28,20},{1,25},{... | collective-permute-start | bytes 196616 | tf_op jit(solution)/shard_map/ppermute | solution.py:376
  121.9 1.5 %collective-permute-start.16 = (bf16[4,64,128]{2,1,0:T(8,128)(2,1)S(1)}, bf16[4,64,128]{2,1,0:T(8,128)(2,1)S(1)}, u32[]{:S(2)}, u32[]{:S(2)}) collective-permute-start(bf16[4,64,128]{2,1,0:T(8,128)(2,1)S(1)} %get-tuple-element.59), channel_id=1, source_target_pairs={{0,28},{4,0},{8,4},{12,8},{16,12},{20,16},{24,20},{28,24},{1,29},{... | collective-permute-start | bytes 196616 | tf_op jit(solution)/shard_map/ppermute | solution.py:376
  123.5 4.4 %inverse.2.refs_8_ = bf16[4,64,64,512]{3,2,1,0:T(8,128)(2,1)} custom-call(bf16[32,512]{1,0:T(8,128)(2,1)S(1)} %copy-done.2, bf16[4,64,128]{2,1,0:T(8,128)(2,1)S(1)} %get-tuple-element.67.refs_0_, bf16[4,64,128]{2,1,0:T(8,128)(2,1)S(1)} %collective-permute-done.23.refs_1_, bf16[4,64,128]{2,1,0:T(8,128)(2,1)S(1)} %collective-permute-done.24.refs_2_, ...), custom_call_target="tpu_custom_call" | custom-call | flops 268435456 | bytes 8388608 | tf_op jit(solution)/shard_map/inverse/pallas_call | solution.py:342
  128.0 4.4 %inverse.3 = bf16[4,64,64,512]{3,2,1,0:T(8,128)(2,1)} custom-call(bf16[32,512]{1,0:T(8,128)(2,1)S(1)} %copy-done.2, bf16[4,64,128]{2,1,0:T(8,128)(2,1)S(1)} %get-tuple-element.52.refs_0_, bf16[4,64,128]{2,1,0:T(8,128)(2,1)S(1)} %collective-permute-done.10.refs_1_, ...), custom_call_target="tpu_custom_call", output_to_operand_aliasing={{}: (9, {})} | custom-call | flops 268435456 | bytes 8388608 | tf_op jit(solution)/shard_map/inverse/pallas_call | solution.py:342
  (45 shorter events, 0.2 us)
Async XLA Ops:
  0.0 2.2 %copy-start = (bf16[4,16,4,16,512]{4,3,2,1,0:T(8,128)(2,1)S(1)}, bf16[4,16,4,16,512]{4,3,2,1,0:T(8,128)(2,1)}, u32[]{:S(2)}) copy-start(bf16[4,16,4,16,512]{4,3,2,1,0:T(8,128)(2,1)} %refs_0_.3) | copy-start | bytes 12582916
  2.2 38.9 %copy-start.10 = (s32[4,16,4]{1,2,0:T(4,128)S(1)}, s32[4,16,4]{1,2,0:T(4,128)}, u32[]{:S(2)}) copy-start(s32[4,16,4]{1,2,0:T(4,128)} %param.8) | copy-start | bytes 3076
  3.4 120.1 %copy-start.2 = (bf16[32,512]{1,0:T(8,128)(2,1)S(1)}, bf16[32,512]{1,0:T(8,128)(2,1)}, u32[]{:S(2)}) copy-start(bf16[32,512]{1,0:T(8,128)(2,1)} %constant.2.clone.cas_ref) | copy-start | bytes 98308
  3.4 51.2 %collective-permute-start.8 = (bf16[4,2,2,4,16,512]{5,4,3,2,1,0:T(8,128)(2,1)}, bf16[4,2,2,4,16,512]{5,4,3,2,1,0:T(8,128)(2,1)S(1)}, u32[]{:S(2)}, u32[]{:S(2)}) collective-permute-start(bf16[4,2,2,4,16,512]{5,4,3,2,1,0:T(8,128)(2,1)} %get-tuple-element.51), channel_id=1, source_target_pairs={{0,1},{1,0},{2,3},{3,2},{4,5},{5,4},{6,7},{7,6},{8,9},{9,8},{10,11... | collective-permute-start | bytes 3145736 | tf_op jit(solution)/shard_map/ppermute | solution.py:386
  14.4 10.3 %collective-permute-start = (bf16[4,2,64,128]{3,2,1,0:T(8,128)(2,1)}, bf16[4,2,64,128]{3,2,1,0:T(8,128)(2,1)S(1)}, u32[]{:S(2)}, u32[]{:S(2)}) collective-permute-start(bf16[4,2,64,128]{3,2,1,0:T(8,128)(2,1)} %get-tuple-element.41), channel_id=1, source_target_pairs={{0,4},{4,8},{8,12},{12,16},{16,20},{20,24},{24,28},{28,0},{1,5},{5... | collective-permute-start | bytes 393224 | tf_op jit(solution)/shard_map/ppermute | solution.py:376
  17.0 8.4 %collective-permute-start.1 = (bf16[4,2,64,128]{3,2,1,0:T(8,128)(2,1)}, bf16[4,2,64,128]{3,2,1,0:T(8,128)(2,1)S(1)}, u32[]{:S(2)}, u32[]{:S(2)}) collective-permute-start(bf16[4,2,64,128]{3,2,1,0:T(8,128)(2,1)} %get-tuple-element.42), channel_id=1, source_target_pairs={{0,8},{4,12},{8,16},{12,20},{16,24},{20,28},{24,0},{28,4},{1,9},{5... | collective-permute-start | bytes 393224 | tf_op jit(solution)/shard_map/ppermute | solution.py:376
  18.6 17.2 %collective-permute-start.2 = (bf16[4,2,64,128]{3,2,1,0:T(8,128)(2,1)}, bf16[4,2,64,128]{3,2,1,0:T(8,128)(2,1)S(1)}, u32[]{:S(2)}, u32[]{:S(2)}) collective-permute-start(bf16[4,2,64,128]{3,2,1,0:T(8,128)(2,1)} %get-tuple-element.43), channel_id=1, source_target_pairs={{0,12},{4,16},{8,20},{12,24},{16,28},{20,0},{24,4},{28,8},{1,13},{... | collective-permute-start | bytes 393224 | tf_op jit(solution)/shard_map/ppermute | solution.py:376
  21.1 20.7 %collective-permute-start.3 = (bf16[4,2,64,128]{3,2,1,0:T(8,128)(2,1)}, bf16[4,2,64,128]{3,2,1,0:T(8,128)(2,1)S(1)}, u32[]{:S(2)}, u32[]{:S(2)}) collective-permute-start(bf16[4,2,64,128]{3,2,1,0:T(8,128)(2,1)} %get-tuple-element.44), channel_id=1, source_target_pairs={{0,16},{4,20},{8,24},{12,28},{16,0},{20,4},{24,8},{28,12},{1,17},{... | collective-permute-start | bytes 393224 | tf_op jit(solution)/shard_map/ppermute | solution.py:376
  24.7 19.2 %copy-start.4 = (bf16[4,2,64,128]{3,2,1,0:T(8,128)(2,1)}, bf16[4,2,64,128]{3,2,1,0:T(8,128)(2,1)S(1)}, u32[]{:S(2)}) copy-start(bf16[4,2,64,128]{3,2,1,0:T(8,128)(2,1)S(1)} %collective-permute-done.refs_1_) | copy-start | bytes 393220
  24.7 17.2 %collective-permute-start.4 = (bf16[4,2,64,128]{3,2,1,0:T(8,128)(2,1)}, bf16[4,2,64,128]{3,2,1,0:T(8,128)(2,1)S(1)}, u32[]{:S(2)}, u32[]{:S(2)}) collective-permute-start(bf16[4,2,64,128]{3,2,1,0:T(8,128)(2,1)} %get-tuple-element.45), channel_id=1, source_target_pairs={{0,20},{4,24},{8,28},{12,0},{16,4},{20,8},{24,12},{28,16},{1,21},{... | collective-permute-start | bytes 393224 | tf_op jit(solution)/shard_map/ppermute | solution.py:376
  25.4 18.5 %copy-start.5 = (bf16[4,2,64,128]{3,2,1,0:T(8,128)(2,1)}, bf16[4,2,64,128]{3,2,1,0:T(8,128)(2,1)S(1)}, u32[]{:S(2)}) copy-start(bf16[4,2,64,128]{3,2,1,0:T(8,128)(2,1)S(1)} %collective-permute-done.1.refs_2_) | copy-start | bytes 393220
  25.4 16.5 %collective-permute-start.5 = (bf16[4,2,64,128]{3,2,1,0:T(8,128)(2,1)}, bf16[4,2,64,128]{3,2,1,0:T(8,128)(2,1)S(1)}, u32[]{:S(2)}, u32[]{:S(2)}) collective-permute-start(bf16[4,2,64,128]{3,2,1,0:T(8,128)(2,1)} %get-tuple-element.46), channel_id=1, source_target_pairs={{0,24},{4,28},{8,0},{12,4},{16,8},{20,12},{24,16},{28,20},{1,25},{... | collective-permute-start | bytes 393224 | tf_op jit(solution)/shard_map/ppermute | solution.py:376
  35.7 8.2 %copy-start.6 = (bf16[4,2,64,128]{3,2,1,0:T(8,128)(2,1)}, bf16[4,2,64,128]{3,2,1,0:T(8,128)(2,1)S(1)}, u32[]{:S(2)}) copy-start(bf16[4,2,64,128]{3,2,1,0:T(8,128)(2,1)S(1)} %collective-permute-done.2.refs_3_) | copy-start | bytes 393220
  35.7 8.2 %collective-permute-start.6 = (bf16[4,2,64,128]{3,2,1,0:T(8,128)(2,1)}, bf16[4,2,64,128]{3,2,1,0:T(8,128)(2,1)}, u32[]{:S(2)}, u32[]{:S(2)}) collective-permute-start(bf16[4,2,64,128]{3,2,1,0:T(8,128)(2,1)} %get-tuple-element.47), channel_id=1, source_target_pairs={{0,28},{4,0},{8,4},{12,8},{16,12},{20,16},{24,20},{28,24},{1,29},{... | collective-permute-start | bytes 393224 | tf_op jit(solution)/shard_map/ppermute | solution.py:376
  41.9 2.1 %copy-start.7 = (bf16[4,2,64,128]{3,2,1,0:T(8,128)(2,1)}, bf16[4,2,64,128]{3,2,1,0:T(8,128)(2,1)S(1)}, u32[]{:S(2)}) copy-start(bf16[4,2,64,128]{3,2,1,0:T(8,128)(2,1)S(1)} %collective-permute-done.3.refs_4_) | copy-start | bytes 393220
  41.9 2.0 %copy-start.8 = (bf16[4,2,64,128]{3,2,1,0:T(8,128)(2,1)}, bf16[4,2,64,128]{3,2,1,0:T(8,128)(2,1)S(1)}, u32[]{:S(2)}) copy-start(bf16[4,2,64,128]{3,2,1,0:T(8,128)(2,1)S(1)} %collective-permute-done.4.refs_5_) | copy-start | bytes 393220
  41.9 2.0 %copy-start.9 = (bf16[4,2,64,128]{3,2,1,0:T(8,128)(2,1)}, bf16[4,2,64,128]{3,2,1,0:T(8,128)(2,1)S(1)}, u32[]{:S(2)}) copy-start(bf16[4,2,64,128]{3,2,1,0:T(8,128)(2,1)S(1)} %collective-permute-done.5.refs_6_) | copy-start | bytes 393220
  48.9 5.7 %collective-permute-start.7 = (bf16[4,2,2,32,128]{4,3,2,1,0:T(8,128)(2,1)}, bf16[4,2,2,32,128]{4,3,2,1,0:T(8,128)(2,1)S(1)}, u32[]{:S(2)}, u32[]{:S(2)}) collective-permute-start(bf16[4,2,2,32,128]{4,3,2,1,0:T(8,128)(2,1)} %get-tuple-element.49), channel_id=1, source_target_pairs={{0,1},{1,0},{2,3},{3,2},{4,5},{5,4},{6,7},{7,6},{8,9},{9,8},{10,11... | collective-permute-start | bytes 393224 | tf_op jit(solution)/shard_map/ppermute | solution.py:386
  51.6 44.0 %collective-permute-start.20 = (bf16[4,2,4,16,512]{4,3,2,1,0:T(8,128)(2,1)}, bf16[4,2,4,16,512]{4,3,2,1,0:T(8,128)(2,1)S(1)}, u32[]{:S(2)}, u32[]{:S(2)}) collective-permute-start(bf16[4,2,4,16,512]{4,3,2,1,0:T(8,128)(2,1)} %get-tuple-element.64), channel_id=1, source_target_pairs={{0,1},{1,2},{2,3},{3,0},{4,5},{5,6},{6,7},{7,4},{8,9},{9,10},{10,1... | collective-permute-start | bytes 1572872 | tf_op jit(solution)/shard_map/ppermute | solution.py:376
  52.1 43.5 %collective-permute-start.21 = (bf16[4,2,4,16,512]{4,3,2,1,0:T(8,128)(2,1)}, bf16[4,2,4,16,512]{4,3,2,1,0:T(8,128)(2,1)S(1)}, u32[]{:S(2)}, u32[]{:S(2)}) collective-permute-start(bf16[4,2,4,16,512]{4,3,2,1,0:T(8,128)(2,1)} %get-tuple-element.65), channel_id=1, source_target_pairs={{0,2},{1,3},{2,0},{3,1},{4,6},{5,7},{6,4},{7,5},{8,10},{9,11},{10,... | collective-permute-start | bytes 1572872 | tf_op jit(solution)/shard_map/ppermute | solution.py:376
  53.6 41.9 %collective-permute-start.22 = (bf16[4,2,4,16,512]{4,3,2,1,0:T(8,128)(2,1)}, bf16[4,2,4,16,512]{4,3,2,1,0:T(8,128)(2,1)S(1)}, u32[]{:S(2)}, u32[]{:S(2)}) collective-permute-start(bf16[4,2,4,16,512]{4,3,2,1,0:T(8,128)(2,1)} %get-tuple-element.66), channel_id=1, source_target_pairs={{0,3},{1,0},{2,1},{3,2},{4,7},{5,4},{6,5},{7,6},{8,11},{9,8},{10,9... | collective-permute-start | bytes 1572872 | tf_op jit(solution)/shard_map/ppermute | solution.py:376
  54.6 0.9 copy-start.1
  55.9 48.1 %collective-permute-start.9 = (bf16[4,2,64,512]{3,2,1,0:T(8,128)(2,1)S(1)}, bf16[4,2,64,512]{3,2,1,0:T(8,128)(2,1)S(1)}, u32[]{:S(2)}, u32[]{:S(2)}) collective-permute-start(bf16[4,2,64,512]{3,2,1,0:T(8,128)(2,1)S(1)} %synthesis.3), channel_id=1, source_target_pairs={{0,2},{1,3},{2,0},{3,1},{4,6},{5,7},{6,4},{7,5},{8,10},{9,11},{10,... | collective-permute-start | bytes 1572872 | tf_op jit(solution)/shard_map/ppermute | solution.py:386
  56.5 32.4 %collective-permute-start.17 = (bf16[4,2,32,128]{3,2,1,0:T(8,128)(2,1)}, bf16[4,2,32,128]{3,2,1,0:T(8,128)(2,1)S(1)}, u32[]{:S(2)}, u32[]{:S(2)}) collective-permute-start(bf16[4,2,32,128]{3,2,1,0:T(8,128)(2,1)} %get-tuple-element.61), channel_id=1, source_target_pairs={{0,1},{1,2},{2,3},{3,0},{4,5},{5,6},{6,7},{7,4},{8,9},{9,10},{10,1... | collective-permute-start | bytes 196616 | tf_op jit(solution)/shard_map/ppermute | solution.py:376
  88.9 4.5 %collective-permute-start.18 = (bf16[4,2,32,128]{3,2,1,0:T(8,128)(2,1)}, bf16[4,2,32,128]{3,2,1,0:T(8,128)(2,1)S(1)}, u32[]{:S(2)}, u32[]{:S(2)}) collective-permute-start(bf16[4,2,32,128]{3,2,1,0:T(8,128)(2,1)} %get-tuple-element.62), channel_id=1, source_target_pairs={{0,2},{1,3},{2,0},{3,1},{4,6},{5,7},{6,4},{7,5},{8,10},{9,11},{10,... | collective-permute-start | bytes 196616 | tf_op jit(solution)/shard_map/ppermute | solution.py:376
  93.3 2.2 %collective-permute-start.19 = (bf16[4,2,32,128]{3,2,1,0:T(8,128)(2,1)}, bf16[4,2,32,128]{3,2,1,0:T(8,128)(2,1)S(1)}, u32[]{:S(2)}, u32[]{:S(2)}) collective-permute-start(bf16[4,2,32,128]{3,2,1,0:T(8,128)(2,1)} %get-tuple-element.63), channel_id=1, source_target_pairs={{0,3},{1,0},{2,1},{3,2},{4,7},{5,4},{6,5},{7,6},{8,11},{9,8},{10,9... | collective-permute-start | bytes 196616 | tf_op jit(solution)/shard_map/ppermute | solution.py:376
  95.6 0.8 copy-start.3
  97.2 10.7 %collective-permute-start.23 = (bf16[4,64,128]{2,1,0:T(8,128)(2,1)S(1)}, bf16[4,64,128]{2,1,0:T(8,128)(2,1)S(1)}, u32[]{:S(2)}, u32[]{:S(2)}) collective-permute-start(bf16[4,64,128]{2,1,0:T(8,128)(2,1)S(1)} %get-tuple-element.68), channel_id=1, source_target_pairs={{0,4},{4,8},{8,12},{12,16},{16,20},{20,24},{24,28},{28,0},{1,5},{5... | collective-permute-start | bytes 196616 | tf_op jit(solution)/shard_map/ppermute | solution.py:376
  97.3 12.0 %collective-permute-start.24 = (bf16[4,64,128]{2,1,0:T(8,128)(2,1)S(1)}, bf16[4,64,128]{2,1,0:T(8,128)(2,1)S(1)}, u32[]{:S(2)}, u32[]{:S(2)}) collective-permute-start(bf16[4,64,128]{2,1,0:T(8,128)(2,1)S(1)} %get-tuple-element.69), channel_id=1, source_target_pairs={{0,8},{4,12},{8,16},{12,20},{16,24},{20,28},{24,0},{28,4},{1,9},{5... | collective-permute-start | bytes 196616 | tf_op jit(solution)/shard_map/ppermute | solution.py:376
  100.7 10.3 %collective-permute-start.25 = (bf16[4,64,128]{2,1,0:T(8,128)(2,1)S(1)}, bf16[4,64,128]{2,1,0:T(8,128)(2,1)S(1)}, u32[]{:S(2)}, u32[]{:S(2)}) collective-permute-start(bf16[4,64,128]{2,1,0:T(8,128)(2,1)S(1)} %get-tuple-element.70), channel_id=1, source_target_pairs={{0,12},{4,16},{8,20},{12,24},{16,28},{20,0},{24,4},{28,8},{1,13},{... | collective-permute-start | bytes 196616 | tf_op jit(solution)/shard_map/ppermute | solution.py:376
  104.0 8.2 %collective-permute-start.26 = (bf16[4,64,128]{2,1,0:T(8,128)(2,1)S(1)}, bf16[4,64,128]{2,1,0:T(8,128)(2,1)S(1)}, u32[]{:S(2)}, u32[]{:S(2)}) collective-permute-start(bf16[4,64,128]{2,1,0:T(8,128)(2,1)S(1)} %get-tuple-element.71), channel_id=1, source_target_pairs={{0,16},{4,20},{8,24},{12,28},{16,0},{20,4},{24,8},{28,12},{1,17},{... | collective-permute-start | bytes 196616 | tf_op jit(solution)/shard_map/ppermute | solution.py:376
  104.0 8.2 %collective-permute-start.27 = (bf16[4,64,128]{2,1,0:T(8,128)(2,1)S(1)}, bf16[4,64,128]{2,1,0:T(8,128)(2,1)S(1)}, u32[]{:S(2)}, u32[]{:S(2)}) collective-permute-start(bf16[4,64,128]{2,1,0:T(8,128)(2,1)S(1)} %get-tuple-element.72), channel_id=1, source_target_pairs={{0,20},{4,24},{8,28},{12,0},{16,4},{20,8},{24,12},{28,16},{1,21},{... | collective-permute-start | bytes 196616 | tf_op jit(solution)/shard_map/ppermute | solution.py:376
  107.9 10.2 %collective-permute-start.28 = (bf16[4,64,128]{2,1,0:T(8,128)(2,1)S(1)}, bf16[4,64,128]{2,1,0:T(8,128)(2,1)S(1)}, u32[]{:S(2)}, u32[]{:S(2)}) collective-permute-start(bf16[4,64,128]{2,1,0:T(8,128)(2,1)S(1)} %get-tuple-element.73), channel_id=1, source_target_pairs={{0,24},{4,28},{8,0},{12,4},{16,8},{20,12},{24,16},{28,20},{1,25},{... | collective-permute-start | bytes 196616 | tf_op jit(solution)/shard_map/ppermute | solution.py:376
  109.3 10.0 %collective-permute-start.29 = (bf16[4,64,128]{2,1,0:T(8,128)(2,1)S(1)}, bf16[4,64,128]{2,1,0:T(8,128)(2,1)S(1)}, u32[]{:S(2)}, u32[]{:S(2)}) collective-permute-start(bf16[4,64,128]{2,1,0:T(8,128)(2,1)S(1)} %get-tuple-element.74), channel_id=1, source_target_pairs={{0,28},{4,0},{8,4},{12,8},{16,12},{20,16},{24,20},{28,24},{1,29},{... | collective-permute-start | bytes 196616 | tf_op jit(solution)/shard_map/ppermute | solution.py:376
  111.0 9.5 %collective-permute-start.10 = (bf16[4,64,128]{2,1,0:T(8,128)(2,1)S(1)}, bf16[4,64,128]{2,1,0:T(8,128)(2,1)S(1)}, u32[]{:S(2)}, u32[]{:S(2)}) collective-permute-start(bf16[4,64,128]{2,1,0:T(8,128)(2,1)S(1)} %get-tuple-element.53), channel_id=1, source_target_pairs={{0,4},{4,8},{8,12},{12,16},{16,20},{20,24},{24,28},{28,0},{1,5},{5... | collective-permute-start | bytes 196616 | tf_op jit(solution)/shard_map/ppermute | solution.py:376
  112.2 9.7 %collective-permute-start.11 = (bf16[4,64,128]{2,1,0:T(8,128)(2,1)S(1)}, bf16[4,64,128]{2,1,0:T(8,128)(2,1)S(1)}, u32[]{:S(2)}, u32[]{:S(2)}) collective-permute-start(bf16[4,64,128]{2,1,0:T(8,128)(2,1)S(1)} %get-tuple-element.54), channel_id=1, source_target_pairs={{0,8},{4,12},{8,16},{12,20},{16,24},{20,28},{24,0},{28,4},{1,9},{5... | collective-permute-start | bytes 196616 | tf_op jit(solution)/shard_map/ppermute | solution.py:376
  112.2 15.7 %collective-permute-start.12 = (bf16[4,64,128]{2,1,0:T(8,128)(2,1)S(1)}, bf16[4,64,128]{2,1,0:T(8,128)(2,1)S(1)}, u32[]{:S(2)}, u32[]{:S(2)}) collective-permute-start(bf16[4,64,128]{2,1,0:T(8,128)(2,1)S(1)} %get-tuple-element.55), channel_id=1, source_target_pairs={{0,12},{4,16},{8,20},{12,24},{16,28},{20,0},{24,4},{28,8},{1,13},{... | collective-permute-start | bytes 196616 | tf_op jit(solution)/shard_map/ppermute | solution.py:376
  118.1 9.8 %collective-permute-start.13 = (bf16[4,64,128]{2,1,0:T(8,128)(2,1)S(1)}, bf16[4,64,128]{2,1,0:T(8,128)(2,1)S(1)}, u32[]{:S(2)}, u32[]{:S(2)}) collective-permute-start(bf16[4,64,128]{2,1,0:T(8,128)(2,1)S(1)} %get-tuple-element.56), channel_id=1, source_target_pairs={{0,16},{4,20},{8,24},{12,28},{16,0},{20,4},{24,8},{28,12},{1,17},{... | collective-permute-start | bytes 196616 | tf_op jit(solution)/shard_map/ppermute | solution.py:376
  119.3 8.6 %collective-permute-start.14 = (bf16[4,64,128]{2,1,0:T(8,128)(2,1)S(1)}, bf16[4,64,128]{2,1,0:T(8,128)(2,1)S(1)}, u32[]{:S(2)}, u32[]{:S(2)}) collective-permute-start(bf16[4,64,128]{2,1,0:T(8,128)(2,1)S(1)} %get-tuple-element.57), channel_id=1, source_target_pairs={{0,20},{4,24},{8,28},{12,0},{16,4},{20,8},{24,12},{28,16},{1,21},{... | collective-permute-start | bytes 196616 | tf_op jit(solution)/shard_map/ppermute | solution.py:376
  120.5 7.5 %collective-permute-start.15 = (bf16[4,64,128]{2,1,0:T(8,128)(2,1)S(1)}, bf16[4,64,128]{2,1,0:T(8,128)(2,1)S(1)}, u32[]{:S(2)}, u32[]{:S(2)}) collective-permute-start(bf16[4,64,128]{2,1,0:T(8,128)(2,1)S(1)} %get-tuple-element.58), channel_id=1, source_target_pairs={{0,24},{4,28},{8,0},{12,4},{16,8},{20,12},{24,16},{28,20},{1,25},{... | collective-permute-start | bytes 196616 | tf_op jit(solution)/shard_map/ppermute | solution.py:376
  121.9 6.0 %collective-permute-start.16 = (bf16[4,64,128]{2,1,0:T(8,128)(2,1)S(1)}, bf16[4,64,128]{2,1,0:T(8,128)(2,1)S(1)}, u32[]{:S(2)}, u32[]{:S(2)}) collective-permute-start(bf16[4,64,128]{2,1,0:T(8,128)(2,1)S(1)} %get-tuple-element.59), channel_id=1, source_target_pairs={{0,28},{4,0},{8,4},{12,8},{16,12},{20,16},{24,20},{28,24},{1,29},{... | collective-permute-start | bytes 196616 | tf_op jit(solution)/shard_map/ppermute | solution.py:376
